TPU v7x, 128 devices: a whole 4x4x4 slice. The times are simulated.
128 devices in a mesh: section: 2 (over z_hi), row: 8 (over x, core), col: 8 (over y, z_lo).
Axes of the slice: x: 4, y: 4, z: 4 (z_hi: 2, z_lo: 2; z = z_hi * 2 + z_lo), core: 2. Of those that a mesh axis runs over, the one named last changes fastest.
Arguments:
- inputs: float32 [3, 128, 16384], P(None, None, ('row', 'col')), may hold values from -512 to 512
- weights: float32 [2, 8, 8, 256, 16384], P('section', None, 'col', None, 'row'), may hold values from -1 to 1
- norm_gain: float32 [2, 16384], P('section', ('row', 'col')), may hold values from 0.5 to 1.5
Outputs:
- section_outputs: float32 [2, 3, 128, 16384], P('section', None, None, ('row', 'col'))
All inputs are finite; a program needn't handle non-finite values.
Results may differ from a plain program's by a relative error of at most 0.00036.
Values sent between devices are 32-bit elements; how exact they have to be, the bound alone decides.
No kernel may reach another device: no remote copies, remote signals or barrier semaphores. Data moves between devices by JAX's collectives and lax.ppermute only.
A program may use at most 128 MiB of HBM per device.

v0:
```python
import jax
import jax.numpy as jnp
from jax import lax
from jax.experimental import pallas as pl
from jax.experimental.pallas import tpu as pltpu
from jax.sharding import PartitionSpec as P


CHUNKS = (128, 128, 128)
D = 16384
F = 256
f32 = jnp.float32
bf16 = jnp.bfloat16
CYCLE = ((4, 1, 2), (1, 2, 4), (2, 4, 1))
RING = ((1, 2), (2, 1))


def ring_partner(pos, mask):
    if mask & 1:
        pos = pos ^ 1
    if mask & 2:
        pos = 3 - pos
    return pos


def col_partner(col, mask):
    return ring_partner(col // 2, mask & 3) * 2 + ((col % 2) ^ (mask >> 2))


def swap_rows(value, masks):
    pairs = [(r, ring_partner(r // 2, masks[r % 2]) * 2 + r % 2) for r in range(8)]
    return lax.ppermute(value, "row", pairs)


def swap_cores(value):
    return lax.ppermute(value, "row", [(r, r ^ 1) for r in range(8)])


def swap_cols(value, masks):
    pairs = [(r * 8 + c, r * 8 + col_partner(c, masks[r % 2])) for r in range(8) for c in range(8)]
    return lax.ppermute(value, ("row", "col"), pairs)


def vmem():
    return pl.BlockSpec(memory_space=pltpu.VMEM)


def smem():
    return pl.BlockSpec(memory_space=pltpu.SMEM)


def call(body, outs, args, scratch=(), limit=4 << 20, scalars=0, flops=0, specs=None):
    return pl.pallas_call(
        body,
        out_shape=[jax.ShapeDtypeStruct(s, t) for s, t in outs],
        in_specs=specs or [smem()] * scalars + [vmem()] * (len(args) - scalars),
        out_specs=[vmem()] * len(outs),
        scratch_shapes=list(scratch),
        compiler_params=pltpu.CompilerParams(vmem_limit_bytes=limit),
        cost_estimate=pl.CostEstimate(flops=flops, transcendentals=0, bytes_accessed=0),
    )(*args)


def split_weights(weights, half):
    block, slots = 128, 4
    count = 1024 // block
    per = F // block

    def body(w, one, two, buf, sems):
        row = lax.axis_index("row")
        x, core = row // 2, row % 2

        def piece(m):
            whose = jnp.where(m < 4, core, 1 - core)
            low, high = m % 2, (m // 2) % 2
            one_flip = jnp.where(whose == 0, low, high)
            two_flip = jnp.where(whose == 0, high, low)
            chip = jnp.where(one_flip == 1, x ^ 1, x)
            chip = jnp.where(two_flip == 1, 3 - chip, chip)
            return chip * 2 + whose

        def fetch(n):
            m = n // per + 4 * half
            source = pl.multiple_of(piece(m) * F + (n % per) * block, block)
            return pltpu.make_async_copy(w.at[pl.ds(source, block)], buf.at[n % slots], sems.at[n % slots])

        for n in range(slots - 1):
            fetch(n).start()

        def step(n, _):
            @pl.when(n + slots - 1 < count)
            def _():
                fetch(n + slots - 1).start()

            fetch(n).wait()

            def rows(i, _):
                value = buf[n % slots, pl.ds(pl.multiple_of(i * 16, 16), 16)]
                first = value.astype(bf16)
                spot = pl.ds(pl.multiple_of(n * block + i * 16, 16), 16)
                one[spot] = first
                two[spot] = (value - first.astype(f32)).astype(bf16)
                return 0

            lax.fori_loop(0, block // 16, rows, 0, unroll=2)
            return 0

        lax.fori_loop(0, count, step, 0)

    shape = (1024, 2048)
    return call(
        body,
        [(shape, bf16)] * 2,
        (pltpu.with_memory_space_constraint(weights, pltpu.HBM),),
        scratch=[pltpu.VMEM((slots, block, 2048), f32), pltpu.SemaphoreType.DMA((slots,))],
        specs=[pl.BlockSpec(memory_space=pltpu.HBM)],
        limit=6 << 20,
        flops=1 << 24,
    )


def rows_to_lanes(total, rows):
    folded = total[:, :128] + total[:, 128:]
    lanes = []
    for start in range(0, rows, 128):
        block = folded[start : start + 128]
        if block.shape[0] < 128:
            block = jnp.concatenate([block, jnp.zeros((128 - block.shape[0], 128), f32)], axis=0)
        lanes.append(jnp.sum(block.T, axis=0, keepdims=True))
    lanes.append(jnp.zeros((8 - len(lanes), 128), f32))
    return jnp.concatenate(lanes, axis=0)


def lanes_to_rows(lanes, rows):
    blocks = []
    for i, start in enumerate(range(0, rows, 128)):
        count = min(128, rows - start)
        block = jnp.broadcast_to(lanes[i : i + 1], (128, 128)).T[:count]
        blocks.append(jnp.concatenate([block, block], axis=1))
    return blocks[0] if len(blocks) == 1 else jnp.concatenate(blocks, axis=0)


def product(orders, own, across, halves, rows, second_layer):
    extra = 8 if second_layer else 0

    def body(p, q, w1, w2, w3, w4, send, keep, lhs):
        core, col = lax.axis_index("row") % 2, lax.axis_index("col")

        def place(slot):
            mask = 0
            for i in range(3):
                dim = jnp.where(core == 0, orders[0][i], orders[1][i])
                mask = mask + ((slot >> (2 - i)) & 1) * dim
            y = col // 2
            y = jnp.where((mask & 1) == 1, y ^ 1, y)
            y = jnp.where((mask & 2) == 2, 3 - y, y)
            return y * 2 + ((col % 2) ^ (mask >> 2))

        total = None
        for m in range(8):
            ref = p.at[m] if m < 4 else q.at[m - 4]
            value = ref[:rows]
            if second_layer:
                total = value * value if total is None else total + value * value
                value = value * ref[rows : rows + 1]
            first = value.astype(bf16)
            lhs[:rows, m * F : (m + 1) * F] = first
            lhs[rows:, m * F : (m + 1) * F] = (value - first.astype(f32)).astype(bf16)

        def step(k, _):
            for target, slot in ((send, k + 4), (keep, k)):
                spot = pl.ds(pl.multiple_of(place(slot) * F, F), F)
                both = jnp.dot(lhs[:, :1024], w1[:, spot], preferred_element_type=f32)
                both = both + jnp.dot(lhs[:, 1024:], w3[:, spot], preferred_element_type=f32)
                other = jnp.dot(lhs[:rows, :1024], w2[:, spot], preferred_element_type=f32)
                other = other + jnp.dot(lhs[:rows, 1024:], w4[:, spot], preferred_element_type=f32)
                target[k, :rows] = both[:rows] + both[rows:] + other
            return 0

        lax.fori_loop(0, 4, step, 0, unroll=2)
        if second_layer:
            lanes = rows_to_lanes(total, rows)
            lanes = jnp.concatenate([lanes, jnp.zeros((8, 128), f32)], axis=1)
            for k in range(4):
                send[k, rows:] = lanes
                keep[k, rows:] = lanes

    return call(
        body,
        [((4, rows + extra, F), f32)] * 2,
        (own, across, *halves),
        scratch=[pltpu.VMEM((2 * rows, 2048), bf16)],
        limit=8 << 20,
        flops=6 * rows * 2048 * 2048,
    )


def add_halves(kept, arrived):
    half = kept.shape[0] // 2

    def body(keep, got, send, rest):
        send[...] = keep[half:] + got[half:]
        rest[...] = keep[:half] + got[:half]

    return call(body, [((half, *kept.shape[1:]), f32)] * 2, (kept, arrived), flops=1 << 20)


def summed(sent, kept, orders):
    for stage in range(3):
        if stage:
            sent, kept = add_halves(kept, arrived)
        arrived = swap_cols(sent, [order[stage] for order in orders])
    return kept, arrived


def gelu(z):
    return 0.5 * z * (1.0 + jnp.tanh(0.7978845608028654 * (z + 0.044715 * (z * z * z))))


def first_end(kept, arrived, gain, rows):
    def body(p, q, g, z, y):
        value = p[0] + q[0]
        z[...] = value
        y[:rows] = gelu(value)
        y[rows:] = jnp.broadcast_to(g[...], (8, F))

    return call(body, [((rows, F), f32), ((rows + 8, F), f32)], (kept, arrived, gain), flops=1 << 22)


def second_end(kept, arrived, before, gain, rows):
    def body(p, q, za, g, out, squares):
        section = lax.axis_index("section")
        lanes = (p[0, rows:] + q[0, rows:])[:, :128]
        scale = lax.rsqrt(lanes_to_rows(lanes, rows) / D + 1e-06)

        @pl.when(section == 0)
        def _():
            out[...] = gelu(za[...]) * scale * g[...]
            squares[...] = jnp.zeros((8, 128), f32)

        @pl.when(section != 0)
        def _():
            y = gelu(za[...] + scale * (p[0, :rows] + q[0, :rows]))
            squares[...] = rows_to_lanes(y * y, rows)
            out[...] = y * g[...]

    return call(
        body, [((rows, F), f32), ((8, 128), f32)], (kept, arrived, before, gain), flops=1 << 22
    )


def finish(values, lanes):
    count = len(values)
    sizes = [v.shape[0] for v in values]

    def body(*refs):
        section = lax.axis_index("section")
        lanes = refs[count]
        out = refs[count + 1]

        @pl.when(section == 0)
        def _():
            start = 0
            for ref, rows in zip(refs, sizes):
                out[start : start + rows] = ref[...]
                start += rows

        @pl.when(section != 0)
        def _():
            total = jnp.sum(lanes[...], axis=0, keepdims=True)
            start, place = 0, 0
            for ref, rows in zip(refs, sizes):
                width = -(-rows // 128)
                part = [total[:, (place + i) * 128 : (place + i + 1) * 128] for i in range(width)]
                scale = lax.rsqrt(lanes_to_rows(jnp.concatenate(part, axis=0), rows) / D + 1e-06)
                out[start : start + rows] = ref[...] * scale
                start += rows
                place += width

    return call(body, [((sum(sizes), F), f32)], (*values, lanes), flops=1 << 20)[0]


def joined(first, second):
    first = first.reshape(-1, *first.shape[-2:])
    second = second.reshape(-1, *second.shape[-2:])
    count = first.shape[0]

    def body(a, b, out):
        out[:count] = a[...]
        out[count:] = b[...]

    shape = (count + second.shape[0], *first.shape[1:])
    return call(body, [(shape, f32)], (first, second), flops=1 << 20)[0]


def gathered(value):
    first = swap_rows(value, [ring[0] for ring in RING])
    pair = joined(value, first)
    second = swap_rows(pair, [ring[1] for ring in RING])
    own = joined(pair, second)
    return own, swap_cores(own)


def chosen(own, moved):
    def body(a, b, out):
        out[...] = jnp.where(lax.axis_index("section") == 0, a[...], b[...])

    return call(body, [(own.shape, f32)], (own, moved))[0]


def pipeline(inputs, weights, norm_gain):
    flat = inputs.reshape(-1, F)
    gain = norm_gain
    halves = split_weights(weights.reshape(2048, 2048), 0)
    halves = halves + split_weights(weights.reshape(2048, 2048), 1)
    orders = [(CYCLE[i % 3], CYCLE[(i + 1) % 3]) for i in range(len(CHUNKS))]
    starts = [sum(CHUNKS[:i]) for i in range(len(CHUNKS))]

    before, branch = [], []
    for i, rows in enumerate(CHUNKS):
        own, across = gathered(flat[starts[i] : starts[i] + rows])
        sent, kept = product(orders[i], own, across, halves, rows, False)
        kept, arrived = summed(sent, kept, orders[i])
        z, y = first_end(kept, arrived, gain, rows)
        before.append(z)
        moved = lax.ppermute(y, "section", [(0, 1)])
        branch.append(chosen(y, moved))
    values, squares = [], []
    for i, rows in enumerate(CHUNKS):
        own, across = gathered(branch[i])
        sent, kept = product(orders[i], own, across, halves, rows, True)
        kept, arrived = summed(sent, kept, orders[i])
        value, square = second_end(kept, arrived, before[i], gain, rows)
        values.append(value)
        squares.append(square[: -(-rows // 128)].reshape(1, -1))
    lanes = jnp.concatenate(squares, axis=1)
    lanes = lax.all_to_all(jnp.broadcast_to(lanes[None], (64, *lanes.shape)), ("row", "col"), 0, 0, tiled=True)
    return finish(values, lanes.reshape(64, -1)).reshape(1, *inputs.shape)


def solution(mesh):
    placed = (
        P(None, None, ("row", "col")),
        P("section", None, "col", None, "row"),
        P("section", ("row", "col")),
    )
    return jax.shard_map(
        pipeline,
        mesh=mesh,
        in_specs=placed,
        out_specs=P("section", None, None, ("row", "col")),
        check_vma=False,
    )
```

profile of v0, /device:TPU:1, one launch (start us, length us, event | category | flops | bytes accessed | tf_op | source)
XLA Modules:
  0.0 165.9 jit_solution(12154172656107365178)
XLA Ops:
  0.0 1.1 slice_bitcast_fusion
  1.1 3.4 %collective-permute-start.26 = (f32[128,256]{1,0:T(8,128)S(1)}, f32[128,256]{1,0:T(8,128)S(1)}, u32[]{:S(2)}, u32[]{:S(2)}) collective-permute-start(f32[128,256]{1,0:T(8,128)S(1)} %get-tuple-element.109), channel_id=1, source_target_pairs={{0,16},{8,56},{16,0},{24,40},{32,48},{40,24},{48,32},{56,8},{1,17}... | collective-permute-start | bytes 393224 | tf_op jit(solution)/shard_map/ppermute | solution.py:32
  4.5 2.4 %collective-permute-done.26 = f32[128,256]{1,0:T(8,128)S(1)} collective-permute-done((f32[128,256]{1,0:T(8,128)S(1)}, f32[128,256]{1,0:T(8,128)S(1)}, u32[]{:S(2)}, u32[]{:S(2)}) %collective-permute-start.26) | collective-permute-done | bytes 131104 | tf_op jit(solution)/shard_map/ppermute | solution.py:32
  7.4 5.0 %collective-permute-done.27.b = f32[2,128,256]{2,1,0:T(8,128)S(1)} collective-permute-done((f32[2,128,256]{2,1,0:T(8,128)S(1)}, f32[2,128,256]{2,1,0:T(8,128)S(1)}, u32[]{:S(2)}, u32[]{:S(2)}) %collective-permute-start.27) | collective-permute-done | bytes 262176 | tf_op jit(solution)/shard_map/ppermute | solution.py:32
  12.5 2.8 %collective-permute-start.28 = (f32[4,128,256]{2,1,0:T(8,128)S(1)}, f32[4,128,256]{2,1,0:T(8,128)S(1)}, u32[]{:S(2)}, u32[]{:S(2)}) collective-permute-start(f32[4,128,256]{2,1,0:T(8,128)S(1)} %shard_map.66.p), channel_id=1, source_target_pairs={{0,8},{8,0},{16,24},{24,16},{32,40},{40,32},{48,56},{56,48},{1,9},... | collective-permute-start | bytes 1572872 | tf_op jit(solution)/shard_map/ppermute | solution.py:36
  15.3 2.6 %collective-permute-start.13 = (f32[128,256]{1,0:T(8,128)S(1)}, f32[128,256]{1,0:T(8,128)S(1)}, u32[]{:S(2)}, u32[]{:S(2)}) collective-permute-start(f32[128,256]{1,0:T(8,128)S(1)} %get-tuple-element.111), channel_id=1, source_target_pairs={{0,16},{8,56},{16,0},{24,40},{32,48},{40,24},{48,32},{56,8},{1,17}... | collective-permute-start | bytes 393224 | tf_op jit(solution)/shard_map/ppermute | solution.py:32
  17.9 2.4 %collective-permute-done.13 = f32[128,256]{1,0:T(8,128)S(1)} collective-permute-done((f32[128,256]{1,0:T(8,128)S(1)}, f32[128,256]{1,0:T(8,128)S(1)}, u32[]{:S(2)}, u32[]{:S(2)}) %collective-permute-start.13) | collective-permute-done | bytes 131104 | tf_op jit(solution)/shard_map/ppermute | solution.py:32
  20.5 2.7 %collective-permute-start = (f32[128,256]{1,0:T(8,128)S(1)}, f32[128,256]{1,0:T(8,128)S(1)}, u32[]{:S(2)}, u32[]{:S(2)}) collective-permute-start(f32[128,256]{1,0:T(8,128)S(1)} %get-tuple-element.110), channel_id=1, source_target_pairs={{0,16},{8,56},{16,0},{24,40},{32,48},{40,24},{48,32},{56,8},{1,17}... | collective-permute-start | bytes 393224 | tf_op jit(solution)/shard_map/ppermute | solution.py:32
  23.1 3.9 %shard_map.39 = (bf16[1024,2048]{1,0:T(8,128)(2,1)S(1)}, bf16[1024,2048]{1,0:T(8,128)(2,1)S(1)}) custom-call(f32[2048,2048]{1,0:T(8,128)} %bitcast.30), custom_call_target="tpu_custom_call" | custom-call | flops 16777216 | tf_op jit(solution)/shard_map/pallas_call | solution.py:53
  27.1 4.0 %shard_map.40 = (bf16[1024,2048]{1,0:T(8,128)(2,1)S(1)}, bf16[1024,2048]{1,0:T(8,128)(2,1)S(1)}) custom-call(f32[2048,2048]{1,0:T(8,128)} %bitcast.31), custom_call_target="tpu_custom_call" | custom-call | flops 16777216 | tf_op jit(solution)/shard_map/pallas_call | solution.py:53
  32.1 3.9 %shard_map.67 = (f32[4,128,256]{2,1,0:T(8,128)S(1)}, f32[4,128,256]{2,1,0:T(8,128)S(1)}) custom-call(f32[4,128,256]{2,1,0:T(8,128)S(1)} %shard_map.66.p, f32[4,128,256]{2,1,0:T(8,128)S(1)} %collective-permute-done.28.q, bf16[1024,2048]{1,0:T(8,128)(2,1)S(1)} %get-tuple-element.57.w1, bf16[1024,2048]{1,0:T(8,128)(2,1)S(1)} %get-tuple-element.58.w2, ...), custom_call_target="tpu_custom_call" | custom-call | flops 3221225472 | tf_op jit(solution)/shard_map/pallas_call | solution.py:53
  36.0 1.7 %collective-permute-start.29 = (f32[4,128,256]{2,1,0:T(8,128)S(1)}, f32[4,128,256]{2,1,0:T(8,128)S(1)}, u32[]{:S(2)}, u32[]{:S(2)}) collective-permute-start(f32[4,128,256]{2,1,0:T(8,128)S(1)} %get-tuple-element.92), channel_id=1, source_target_pairs={{0,6},{1,7},{2,4},{3,5},{4,2},{5,3},{6,0},{7,1},{8,9},{9,8},{10,11... | collective-permute-start | bytes 1572872 | tf_op jit(solution)/shard_map/ppermute | solution.py:41
  37.8 1.9 %collective-permute-start.2 = (f32[4,128,256]{2,1,0:T(8,128)S(1)}, f32[4,128,256]{2,1,0:T(8,128)S(1)}, u32[]{:S(2)}, u32[]{:S(2)}) collective-permute-start(f32[4,128,256]{2,1,0:T(8,128)S(1)} %shard_map.38.p), channel_id=1, source_target_pairs={{0,8},{8,0},{16,24},{24,16},{32,40},{40,32},{48,56},{56,48},{1,9},... | collective-permute-start | bytes 1572872 | tf_op jit(solution)/shard_map/ppermute | solution.py:36
  39.7 3.9 %shard_map.54 = (f32[4,128,256]{2,1,0:T(8,128)S(1)}, f32[4,128,256]{2,1,0:T(8,128)S(1)}) custom-call(f32[4,128,256]{2,1,0:T(8,128)S(1)} %shard_map.53.p, f32[4,128,256]{2,1,0:T(8,128)S(1)} %collective-permute-done.15.q, bf16[1024,2048]{1,0:T(8,128)(2,1)S(1)} %get-tuple-element.57.w1, bf16[1024,2048]{1,0:T(8,128)(2,1)S(1)} %get-tuple-element.58.w2, ...), custom_call_target="tpu_custom_call" | custom-call | flops 3221225472 | tf_op jit(solution)/shard_map/pallas_call | solution.py:53
  43.6 2.2 %collective-permute-start.16 = (f32[4,128,256]{2,1,0:T(8,128)S(1)}, f32[4,128,256]{2,1,0:T(8,128)S(1)}, u32[]{:S(2)}, u32[]{:S(2)}) collective-permute-start(f32[4,128,256]{2,1,0:T(8,128)S(1)} %get-tuple-element.77), channel_id=1, source_target_pairs={{0,2},{1,3},{2,0},{3,1},{4,6},{5,7},{6,4},{7,5},{8,14},{9,15},{10,... | collective-permute-start | bytes 1572872 | tf_op jit(solution)/shard_map/ppermute | solution.py:41
  46.0 3.9 %shard_map.41 = (f32[4,128,256]{2,1,0:T(8,128)S(1)}, f32[4,128,256]{2,1,0:T(8,128)S(1)}) custom-call(f32[4,128,256]{2,1,0:T(8,128)S(1)} %shard_map.38.p, f32[4,128,256]{2,1,0:T(8,128)S(1)} %collective-permute-done.2.q, bf16[1024,2048]{1,0:T(8,128)(2,1)S(1)} %get-tuple-element.57.w1, bf16[1024,2048]{1,0:T(8,128)(2,1)S(1)} %get-tuple-element.58.w2, ...), custom_call_target="tpu_custom_call" | custom-call | flops 3221225472 | tf_op jit(solution)/shard_map/pallas_call | solution.py:53
  49.9 1.5 collective-permute-start.3
  51.4 2.9 %collective-permute-done.30.got = f32[2,128,256]{2,1,0:T(8,128)S(1)} collective-permute-done((f32[2,128,256]{2,1,0:T(8,128)S(1)}, f32[2,128,256]{2,1,0:T(8,128)S(1)}, u32[]{:S(2)}, u32[]{:S(2)}) %collective-permute-start.30) | collective-permute-done | bytes 262176 | tf_op jit(solution)/shard_map/ppermute | solution.py:41
  54.3 1.6 collective-permute-start.31
  56.0 1.5 collective-permute-start.17
  57.5 1.9 %collective-permute-done.31.q = f32[1,128,256]{2,1,0:T(8,128)S(1)} collective-permute-done((f32[1,128,256]{2,1,0:T(8,128)S(1)}, f32[1,128,256]{2,1,0:T(8,128)S(1)}, u32[]{:S(2)}, u32[]{:S(2)}) %collective-permute-start.31) | collective-permute-done | bytes 131104 | tf_op jit(solution)/shard_map/ppermute | solution.py:41
  59.5 5.5 %collective-permute-start.32 = (f32[136,256]{1,0:T(8,128)S(1)}, f32[136,256]{1,0:T(8,128)S(1)}, u32[]{:S(2)}, u32[]{:S(2)}) collective-permute-start(f32[136,256]{1,0:T(8,128)S(1)} %get-tuple-element.97.a), channel_id=1, source_target_pairs={{0,64},{1,65},{2,66},{3,67},{4,68},{5,69},{6,70},{7,71},{8,72},{9,... | collective-permute-start | bytes 417800 | tf_op jit(solution)/shard_map/ppermute | solution.py:326
  65.0 2.4 %collective-permute-done.32.b = f32[136,256]{1,0:T(8,128)S(1)} collective-permute-done((f32[136,256]{1,0:T(8,128)S(1)}, f32[136,256]{1,0:T(8,128)S(1)}, u32[]{:S(2)}, u32[]{:S(2)}) %collective-permute-start.32) | collective-permute-done | bytes 139296 | tf_op jit(solution)/shard_map/ppermute | solution.py:326
  68.2 2.8 %collective-permute-start.4 = (f32[2,128,256]{2,1,0:T(8,128)S(1)}, f32[2,128,256]{2,1,0:T(8,128)S(1)}, u32[]{:S(2)}, u32[]{:S(2)}) collective-permute-start(f32[2,128,256]{2,1,0:T(8,128)S(1)} %get-tuple-element.64), channel_id=1, source_target_pairs={{0,2},{1,3},{2,0},{3,1},{4,6},{5,7},{6,4},{7,5},{8,14},{9,15},{10,... | collective-permute-start | bytes 786440 | tf_op jit(solution)/shard_map/ppermute | solution.py:41
  71.1 1.5 collective-permute-done.33
  72.7 3.9 %collective-permute-done.18.q = f32[1,128,256]{2,1,0:T(8,128)S(1)} collective-permute-done((f32[1,128,256]{2,1,0:T(8,128)S(1)}, f32[1,128,256]{2,1,0:T(8,128)S(1)}, u32[]{:S(2)}, u32[]{:S(2)}) %collective-permute-start.18) | collective-permute-done | bytes 131104 | tf_op jit(solution)/shard_map/ppermute | solution.py:41
  76.7 5.3 %collective-permute-start.19 = (f32[136,256]{1,0:T(8,128)S(1)}, f32[136,256]{1,0:T(8,128)S(1)}, u32[]{:S(2)}, u32[]{:S(2)}) collective-permute-start(f32[136,256]{1,0:T(8,128)S(1)} %get-tuple-element.82.a), channel_id=1, source_target_pairs={{0,64},{1,65},{2,66},{3,67},{4,68},{5,69},{6,70},{7,71},{8,72},{9,... | collective-permute-start | bytes 417800 | tf_op jit(solution)/shard_map/ppermute | solution.py:326
  82.5 2.4 %collective-permute-done.19.b = f32[136,256]{1,0:T(8,128)S(1)} collective-permute-done((f32[136,256]{1,0:T(8,128)S(1)}, f32[136,256]{1,0:T(8,128)S(1)}, u32[]{:S(2)}, u32[]{:S(2)}) %collective-permute-start.19) | collective-permute-done | bytes 139296 | tf_op jit(solution)/shard_map/ppermute | solution.py:326
  85.1 2.1 %collective-permute-done.5.q = f32[1,128,256]{2,1,0:T(8,128)S(1)} collective-permute-done((f32[1,128,256]{2,1,0:T(8,128)S(1)}, f32[1,128,256]{2,1,0:T(8,128)S(1)}, u32[]{:S(2)}, u32[]{:S(2)}) %collective-permute-start.5) | collective-permute-done | bytes 131104 | tf_op jit(solution)/shard_map/ppermute | solution.py:41
  87.3 3.5 %collective-permute-start.6 = (f32[136,256]{1,0:T(8,128)S(1)}, f32[136,256]{1,0:T(8,128)S(1)}, u32[]{:S(2)}, u32[]{:S(2)}) collective-permute-start(f32[136,256]{1,0:T(8,128)S(1)} %get-tuple-element.67.a), channel_id=1, source_target_pairs={{0,64},{1,65},{2,66},{3,67},{4,68},{5,69},{6,70},{7,71},{8,72},{9,... | collective-permute-start | bytes 417800 | tf_op jit(solution)/shard_map/ppermute | solution.py:326
  90.9 3.5 %collective-permute-start.35 = (f32[4,136,256]{2,1,0:T(8,128)S(1)}, f32[4,136,256]{2,1,0:T(8,128)S(1)}, u32[]{:S(2)}, u32[]{:S(2)}) collective-permute-start(f32[4,136,256]{2,1,0:T(8,128)S(1)} %shard_map.73.p), channel_id=1, source_target_pairs={{0,8},{8,0},{16,24},{24,16},{32,40},{40,32},{48,56},{56,48},{1,9},... | collective-permute-start | bytes 1671176 | tf_op jit(solution)/shard_map/ppermute | solution.py:36
  94.7 2.0 %collective-permute-start.7 = (f32[136,256]{1,0:T(8,128)S(1)}, f32[136,256]{1,0:T(8,128)S(1)}, u32[]{:S(2)}, u32[]{:S(2)}) collective-permute-start(f32[136,256]{1,0:T(8,128)S(1)} %shard_map.45), channel_id=1, source_target_pairs={{0,16},{8,56},{16,0},{24,40},{32,48},{40,24},{48,32},{56,8},{1,17}... | collective-permute-start | bytes 417800 | tf_op jit(solution)/shard_map/ppermute | solution.py:32
  96.7 4.8 %collective-permute-done.7 = f32[136,256]{1,0:T(8,128)S(1)} collective-permute-done((f32[136,256]{1,0:T(8,128)S(1)}, f32[136,256]{1,0:T(8,128)S(1)}, u32[]{:S(2)}, u32[]{:S(2)}) %collective-permute-start.7) | collective-permute-done | bytes 139296 | tf_op jit(solution)/shard_map/ppermute | solution.py:32
  101.9 1.8 %collective-permute-start.22 = (f32[4,136,256]{2,1,0:T(8,128)S(1)}, f32[4,136,256]{2,1,0:T(8,128)S(1)}, u32[]{:S(2)}, u32[]{:S(2)}) collective-permute-start(f32[4,136,256]{2,1,0:T(8,128)S(1)} %shard_map.60.p), channel_id=1, source_target_pairs={{0,8},{8,0},{16,24},{24,16},{32,40},{40,32},{48,56},{56,48},{1,9},... | collective-permute-start | bytes 1671176 | tf_op jit(solution)/shard_map/ppermute | solution.py:36
  103.7 3.6 %collective-permute-done.8.b = f32[2,136,256]{2,1,0:T(8,128)S(1)} collective-permute-done((f32[2,136,256]{2,1,0:T(8,128)S(1)}, f32[2,136,256]{2,1,0:T(8,128)S(1)}, u32[]{:S(2)}, u32[]{:S(2)}) %collective-permute-start.8) | collective-permute-done | bytes 278560 | tf_op jit(solution)/shard_map/ppermute | solution.py:32
  107.3 2.7 %collective-permute-start.9 = (f32[4,136,256]{2,1,0:T(8,128)S(1)}, f32[4,136,256]{2,1,0:T(8,128)S(1)}, u32[]{:S(2)}, u32[]{:S(2)}) collective-permute-start(f32[4,136,256]{2,1,0:T(8,128)S(1)} %shard_map.47.p), channel_id=1, source_target_pairs={{0,8},{8,0},{16,24},{24,16},{32,40},{40,32},{48,56},{56,48},{1,9},... | collective-permute-start | bytes 1671176 | tf_op jit(solution)/shard_map/ppermute | solution.py:36
  110.1 4.0 %shard_map.74 = (f32[4,136,256]{2,1,0:T(8,128)S(1)}, f32[4,136,256]{2,1,0:T(8,128)S(1)}) custom-call(f32[4,136,256]{2,1,0:T(8,128)S(1)} %shard_map.73.p, f32[4,136,256]{2,1,0:T(8,128)S(1)} %collective-permute-done.35.q, bf16[1024,2048]{1,0:T(8,128)(2,1)S(1)} %get-tuple-element.57.w1, bf16[1024,2048]{1,0:T(8,128)(2,1)S(1)} %get-tuple-element.58.w2, ...), custom_call_target="tpu_custom_call" | custom-call | flops 3221225472 | tf_op jit(solution)/shard_map/pallas_call | solution.py:53
  114.6 4.0 %shard_map.61 = (f32[4,136,256]{2,1,0:T(8,128)S(1)}, f32[4,136,256]{2,1,0:T(8,128)S(1)}) custom-call(f32[4,136,256]{2,1,0:T(8,128)S(1)} %shard_map.60.p, f32[4,136,256]{2,1,0:T(8,128)S(1)} %collective-permute-done.22.q, bf16[1024,2048]{1,0:T(8,128)(2,1)S(1)} %get-tuple-element.57.w1, bf16[1024,2048]{1,0:T(8,128)(2,1)S(1)} %get-tuple-element.58.w2, ...), custom_call_target="tpu_custom_call" | custom-call | flops 3221225472 | tf_op jit(solution)/shard_map/pallas_call | solution.py:53
  118.7 2.3 %collective-permute-start.23 = (f32[4,136,256]{2,1,0:T(8,128)S(1)}, f32[4,136,256]{2,1,0:T(8,128)S(1)}, u32[]{:S(2)}, u32[]{:S(2)}) collective-permute-start(f32[4,136,256]{2,1,0:T(8,128)S(1)} %get-tuple-element.84), channel_id=1, source_target_pairs={{0,2},{1,3},{2,0},{3,1},{4,6},{5,7},{6,4},{7,5},{8,14},{9,15},{10,... | collective-permute-start | bytes 1671176 | tf_op jit(solution)/shard_map/ppermute | solution.py:41
  121.0 4.0 %shard_map.48 = (f32[4,136,256]{2,1,0:T(8,128)S(1)}, f32[4,136,256]{2,1,0:T(8,128)S(1)}) custom-call(f32[4,136,256]{2,1,0:T(8,128)S(1)} %shard_map.47.p, f32[4,136,256]{2,1,0:T(8,128)S(1)} %collective-permute-done.9.q, bf16[1024,2048]{1,0:T(8,128)(2,1)S(1)} %get-tuple-element.57.w1, bf16[1024,2048]{1,0:T(8,128)(2,1)S(1)} %get-tuple-element.58.w2, ...), custom_call_target="tpu_custom_call" | custom-call | flops 3221225472 | tf_op jit(solution)/shard_map/pallas_call | solution.py:53
  125.6 1.2 collective-permute-start.37
  126.7 3.5 %collective-permute-done.23.got = f32[4,136,256]{2,1,0:T(8,128)S(1)} collective-permute-done((f32[4,136,256]{2,1,0:T(8,128)S(1)}, f32[4,136,256]{2,1,0:T(8,128)S(1)}, u32[]{:S(2)}, u32[]{:S(2)}) %collective-permute-start.23) | collective-permute-done | bytes 557088 | tf_op jit(solution)/shard_map/ppermute | solution.py:41
  130.8 5.6 %collective-permute-done.10.got = f32[4,136,256]{2,1,0:T(8,128)S(1)} collective-permute-done((f32[4,136,256]{2,1,0:T(8,128)S(1)}, f32[4,136,256]{2,1,0:T(8,128)S(1)}, u32[]{:S(2)}, u32[]{:S(2)}) %collective-permute-start.10) | collective-permute-done | bytes 557088 | tf_op jit(solution)/shard_map/ppermute | solution.py:41
  136.6 2.8 %collective-permute-done.37.got = f32[2,136,256]{2,1,0:T(8,128)S(1)} collective-permute-done((f32[2,136,256]{2,1,0:T(8,128)S(1)}, f32[2,136,256]{2,1,0:T(8,128)S(1)}, u32[]{:S(2)}, u32[]{:S(2)}) %collective-permute-start.37) | collective-permute-done | bytes 278560 | tf_op jit(solution)/shard_map/ppermute | solution.py:41
  140.0 3.6 %collective-permute-done.11.got = f32[2,136,256]{2,1,0:T(8,128)S(1)} collective-permute-done((f32[2,136,256]{2,1,0:T(8,128)S(1)}, f32[2,136,256]{2,1,0:T(8,128)S(1)}, u32[]{:S(2)}, u32[]{:S(2)}) %collective-permute-start.11) | collective-permute-done | bytes 278560 | tf_op jit(solution)/shard_map/ppermute | solution.py:41
  143.7 1.4 collective-permute-done.38.q
  145.5 3.7 %collective-permute-done.12.q = f32[1,136,256]{2,1,0:T(8,128)S(1)} collective-permute-done((f32[1,136,256]{2,1,0:T(8,128)S(1)}, f32[1,136,256]{2,1,0:T(8,128)S(1)}, u32[]{:S(2)}, u32[]{:S(2)}) %collective-permute-start.12) | collective-permute-done | bytes 139296 | tf_op jit(solution)/shard_map/ppermute | solution.py:41
  149.5 15.6 %all_to_all.5 = f32[64,1,384]{2,1,0:T(1,128)S(1)} all-to-all(f32[64,1,384]{2,1,0:T(1,128)S(1)} %broadcast_in_dim.9), channel_id=1, replica_groups=mesh['section'=2,'row'=8,'col'=8] {'row','col'}, dimensions={0} | all-to-all | bytes 196608 | tf_op jit(solution)/shard_map/all_to_all | solution.py:337
  (82 shorter events, 8.7 us)
Async XLA Ops:
  1.1 5.7 %collective-permute-start.26 = (f32[128,256]{1,0:T(8,128)S(1)}, f32[128,256]{1,0:T(8,128)S(1)}, u32[]{:S(2)}, u32[]{:S(2)}) collective-permute-start(f32[128,256]{1,0:T(8,128)S(1)} %get-tuple-element.109), channel_id=1, source_target_pairs={{0,16},{8,56},{16,0},{24,40},{32,48},{40,24},{48,32},{56,8},{1,17}... | collective-permute-start | bytes 393224 | tf_op jit(solution)/shard_map/ppermute | solution.py:32
  6.8 5.6 %collective-permute-start.27 = (f32[2,128,256]{2,1,0:T(8,128)S(1)}, f32[2,128,256]{2,1,0:T(8,128)S(1)}, u32[]{:S(2)}, u32[]{:S(2)}) collective-permute-start(f32[2,128,256]{2,1,0:T(8,128)S(1)} %shard_map.65.a), channel_id=1, source_target_pairs={{0,48},{8,24},{16,32},{24,8},{32,16},{40,56},{48,0},{56,40},{1,49}... | collective-permute-start | bytes 786440 | tf_op jit(solution)/shard_map/ppermute | solution.py:32
  12.5 19.6 %collective-permute-start.28 = (f32[4,128,256]{2,1,0:T(8,128)S(1)}, f32[4,128,256]{2,1,0:T(8,128)S(1)}, u32[]{:S(2)}, u32[]{:S(2)}) collective-permute-start(f32[4,128,256]{2,1,0:T(8,128)S(1)} %shard_map.66.p), channel_id=1, source_target_pairs={{0,8},{8,0},{16,24},{24,16},{32,40},{40,32},{48,56},{56,48},{1,9},... | collective-permute-start | bytes 1572872 | tf_op jit(solution)/shard_map/ppermute | solution.py:36
  15.3 5.0 %collective-permute-start.13 = (f32[128,256]{1,0:T(8,128)S(1)}, f32[128,256]{1,0:T(8,128)S(1)}, u32[]{:S(2)}, u32[]{:S(2)}) collective-permute-start(f32[128,256]{1,0:T(8,128)S(1)} %get-tuple-element.111), channel_id=1, source_target_pairs={{0,16},{8,56},{16,0},{24,40},{32,48},{40,24},{48,32},{56,8},{1,17}... | collective-permute-start | bytes 393224 | tf_op jit(solution)/shard_map/ppermute | solution.py:32
  20.4 11.6 %collective-permute-start.14 = (f32[2,128,256]{2,1,0:T(8,128)S(1)}, f32[2,128,256]{2,1,0:T(8,128)S(1)}, u32[]{:S(2)}, u32[]{:S(2)}) collective-permute-start(f32[2,128,256]{2,1,0:T(8,128)S(1)} %shard_map.52.a), channel_id=1, source_target_pairs={{0,48},{8,24},{16,32},{24,8},{32,16},{40,56},{48,0},{56,40},{1,49}... | collective-permute-start | bytes 786440 | tf_op jit(solution)/shard_map/ppermute | solution.py:32
  20.5 10.6 %collective-permute-start = (f32[128,256]{1,0:T(8,128)S(1)}, f32[128,256]{1,0:T(8,128)S(1)}, u32[]{:S(2)}, u32[]{:S(2)}) collective-permute-start(f32[128,256]{1,0:T(8,128)S(1)} %get-tuple-element.110), channel_id=1, source_target_pairs={{0,16},{8,56},{16,0},{24,40},{32,48},{40,24},{48,32},{56,8},{1,17}... | collective-permute-start | bytes 393224 | tf_op jit(solution)/shard_map/ppermute | solution.py:32
  31.1 6.6 %collective-permute-start.1 = (f32[2,128,256]{2,1,0:T(8,128)S(1)}, f32[2,128,256]{2,1,0:T(8,128)S(1)}, u32[]{:S(2)}, u32[]{:S(2)}) collective-permute-start(f32[2,128,256]{2,1,0:T(8,128)S(1)} %shard_map.37.a), channel_id=1, source_target_pairs={{0,48},{8,24},{16,32},{24,8},{32,16},{40,56},{48,0},{56,40},{1,49}... | collective-permute-start | bytes 786440 | tf_op jit(solution)/shard_map/ppermute | solution.py:32
  32.0 7.7 %collective-permute-start.15 = (f32[4,128,256]{2,1,0:T(8,128)S(1)}, f32[4,128,256]{2,1,0:T(8,128)S(1)}, u32[]{:S(2)}, u32[]{:S(2)}) collective-permute-start(f32[4,128,256]{2,1,0:T(8,128)S(1)} %shard_map.53.p), channel_id=1, source_target_pairs={{0,8},{8,0},{16,24},{24,16},{32,40},{40,32},{48,56},{56,48},{1,9},... | collective-permute-start | bytes 1572872 | tf_op jit(solution)/shard_map/ppermute | solution.py:36
  36.0 9.8 %collective-permute-start.29 = (f32[4,128,256]{2,1,0:T(8,128)S(1)}, f32[4,128,256]{2,1,0:T(8,128)S(1)}, u32[]{:S(2)}, u32[]{:S(2)}) collective-permute-start(f32[4,128,256]{2,1,0:T(8,128)S(1)} %get-tuple-element.92), channel_id=1, source_target_pairs={{0,6},{1,7},{2,4},{3,5},{4,2},{5,3},{6,0},{7,1},{8,9},{9,8},{10,11... | collective-permute-start | bytes 1572872 | tf_op jit(solution)/shard_map/ppermute | solution.py:41
  37.8 8.3 %collective-permute-start.2 = (f32[4,128,256]{2,1,0:T(8,128)S(1)}, f32[4,128,256]{2,1,0:T(8,128)S(1)}, u32[]{:S(2)}, u32[]{:S(2)}) collective-permute-start(f32[4,128,256]{2,1,0:T(8,128)S(1)} %shard_map.38.p), channel_id=1, source_target_pairs={{0,8},{8,0},{16,24},{24,16},{32,40},{40,32},{48,56},{56,48},{1,9},... | collective-permute-start | bytes 1572872 | tf_op jit(solution)/shard_map/ppermute | solution.py:36
  43.6 12.3 %collective-permute-start.16 = (f32[4,128,256]{2,1,0:T(8,128)S(1)}, f32[4,128,256]{2,1,0:T(8,128)S(1)}, u32[]{:S(2)}, u32[]{:S(2)}) collective-permute-start(f32[4,128,256]{2,1,0:T(8,128)S(1)} %get-tuple-element.77), channel_id=1, source_target_pairs={{0,2},{1,3},{2,0},{3,1},{4,6},{5,7},{6,4},{7,5},{8,14},{9,15},{10,... | collective-permute-start | bytes 1572872 | tf_op jit(solution)/shard_map/ppermute | solution.py:41
  45.9 13.6 %copy-start = (f32[1,256]{1,0:T(1,128)S(1)}, f32[1,256]{1,0:T(1,128)}, u32[]{:S(2)}) copy-start(f32[1,256]{1,0:T(1,128)} %g.11) | copy-start | bytes 3076
  45.9 8.4 %collective-permute-start.30 = (f32[2,128,256]{2,1,0:T(8,128)S(1)}, f32[2,128,256]{2,1,0:T(8,128)S(1)}, u32[]{:S(2)}, u32[]{:S(2)}) collective-permute-start(f32[2,128,256]{2,1,0:T(8,128)S(1)} %get-tuple-element.94), channel_id=1, source_target_pairs={{0,1},{1,0},{2,3},{3,2},{4,5},{5,4},{6,7},{7,6},{8,10},{9,11},{10,... | collective-permute-start | bytes 786440 | tf_op jit(solution)/shard_map/ppermute | solution.py:41
  49.9 18.2 %collective-permute-start.3 = (f32[4,128,256]{2,1,0:T(8,128)S(1)}, f32[4,128,256]{2,1,0:T(8,128)S(1)}, u32[]{:S(2)}, u32[]{:S(2)}) collective-permute-start(f32[4,128,256]{2,1,0:T(8,128)S(1)} %get-tuple-element.62), channel_id=1, source_target_pairs={{0,1},{1,0},{2,3},{3,2},{4,5},{5,4},{6,7},{7,6},{8,10},{9,11},{10,... | collective-permute-start | bytes 1572872 | tf_op jit(solution)/shard_map/ppermute | solution.py:41
  54.3 5.1 %collective-permute-start.31 = (f32[1,128,256]{2,1,0:T(8,128)S(1)}, f32[1,128,256]{2,1,0:T(8,128)S(1)}, u32[]{:S(2)}, u32[]{:S(2)}) collective-permute-start(f32[1,128,256]{2,1,0:T(8,128)S(1)} %get-tuple-element.96), channel_id=1, source_target_pairs={{0,2},{1,3},{2,0},{3,1},{4,6},{5,7},{6,4},{7,5},{8,14},{9,15},{10,... | collective-permute-start | bytes 393224 | tf_op jit(solution)/shard_map/ppermute | solution.py:41
  56.0 15.0 %collective-permute-start.17 = (f32[2,128,256]{2,1,0:T(8,128)S(1)}, f32[2,128,256]{2,1,0:T(8,128)S(1)}, u32[]{:S(2)}, u32[]{:S(2)}) collective-permute-start(f32[2,128,256]{2,1,0:T(8,128)S(1)} %get-tuple-element.79), channel_id=1, source_target_pairs={{0,6},{1,7},{2,4},{3,5},{4,2},{5,3},{6,0},{7,1},{8,9},{9,8},{10,11... | collective-permute-start | bytes 786440 | tf_op jit(solution)/shard_map/ppermute | solution.py:41
  59.5 7.9 %collective-permute-start.32 = (f32[136,256]{1,0:T(8,128)S(1)}, f32[136,256]{1,0:T(8,128)S(1)}, u32[]{:S(2)}, u32[]{:S(2)}) collective-permute-start(f32[136,256]{1,0:T(8,128)S(1)} %get-tuple-element.97.a), channel_id=1, source_target_pairs={{0,64},{1,65},{2,66},{3,67},{4,68},{5,69},{6,70},{7,71},{8,72},{9,... | collective-permute-start | bytes 417800 | tf_op jit(solution)/shard_map/ppermute | solution.py:326
  67.4 5.2 %collective-permute-start.33 = (f32[136,256]{1,0:T(8,128)S(1)}, f32[136,256]{1,0:T(8,128)S(1)}, u32[]{:S(2)}, u32[]{:S(2)}) collective-permute-start(f32[136,256]{1,0:T(8,128)S(1)} %shard_map.71), channel_id=1, source_target_pairs={{0,16},{8,56},{16,0},{24,40},{32,48},{40,24},{48,32},{56,8},{1,17}... | collective-permute-start | bytes 417800 | tf_op jit(solution)/shard_map/ppermute | solution.py:32
  68.2 13.7 %collective-permute-start.4 = (f32[2,128,256]{2,1,0:T(8,128)S(1)}, f32[2,128,256]{2,1,0:T(8,128)S(1)}, u32[]{:S(2)}, u32[]{:S(2)}) collective-permute-start(f32[2,128,256]{2,1,0:T(8,128)S(1)} %get-tuple-element.64), channel_id=1, source_target_pairs={{0,2},{1,3},{2,0},{3,1},{4,6},{5,7},{6,4},{7,5},{8,14},{9,15},{10,... | collective-permute-start | bytes 786440 | tf_op jit(solution)/shard_map/ppermute | solution.py:41
  71.0 5.6 %collective-permute-start.18 = (f32[1,128,256]{2,1,0:T(8,128)S(1)}, f32[1,128,256]{2,1,0:T(8,128)S(1)}, u32[]{:S(2)}, u32[]{:S(2)}) collective-permute-start(f32[1,128,256]{2,1,0:T(8,128)S(1)} %get-tuple-element.81), channel_id=1, source_target_pairs={{0,1},{1,0},{2,3},{3,2},{4,5},{5,4},{6,7},{7,6},{8,10},{9,11},{10,... | collective-permute-start | bytes 393224 | tf_op jit(solution)/shard_map/ppermute | solution.py:41
  72.6 18.2 %collective-permute-start.34 = (f32[2,136,256]{2,1,0:T(8,128)S(1)}, f32[2,136,256]{2,1,0:T(8,128)S(1)}, u32[]{:S(2)}, u32[]{:S(2)}) collective-permute-start(f32[2,136,256]{2,1,0:T(8,128)S(1)} %shard_map.72.a), channel_id=1, source_target_pairs={{0,48},{8,24},{16,32},{24,8},{32,16},{40,56},{48,0},{56,40},{1,49}... | collective-permute-start | bytes 835592 | tf_op jit(solution)/shard_map/ppermute | solution.py:32
  76.7 8.2 %collective-permute-start.19 = (f32[136,256]{1,0:T(8,128)S(1)}, f32[136,256]{1,0:T(8,128)S(1)}, u32[]{:S(2)}, u32[]{:S(2)}) collective-permute-start(f32[136,256]{1,0:T(8,128)S(1)} %get-tuple-element.82.a), channel_id=1, source_target_pairs={{0,64},{1,65},{2,66},{3,67},{4,68},{5,69},{6,70},{7,71},{8,72},{9,... | collective-permute-start | bytes 417800 | tf_op jit(solution)/shard_map/ppermute | solution.py:326
  82.0 5.2 %collective-permute-start.5 = (f32[1,128,256]{2,1,0:T(8,128)S(1)}, f32[1,128,256]{2,1,0:T(8,128)S(1)}, u32[]{:S(2)}, u32[]{:S(2)}) collective-permute-start(f32[1,128,256]{2,1,0:T(8,128)S(1)} %get-tuple-element.66), channel_id=1, source_target_pairs={{0,6},{1,7},{2,4},{3,5},{4,2},{5,3},{6,0},{7,1},{8,9},{9,8},{10,11... | collective-permute-start | bytes 393224 | tf_op jit(solution)/shard_map/ppermute | solution.py:41
  84.8 9.6 %collective-permute-start.20 = (f32[136,256]{1,0:T(8,128)S(1)}, f32[136,256]{1,0:T(8,128)S(1)}, u32[]{:S(2)}, u32[]{:S(2)}) collective-permute-start(f32[136,256]{1,0:T(8,128)S(1)} %shard_map.58), channel_id=1, source_target_pairs={{0,16},{8,56},{16,0},{24,40},{32,48},{40,24},{48,32},{56,8},{1,17}... | collective-permute-start | bytes 417800 | tf_op jit(solution)/shard_map/ppermute | solution.py:32
  87.3 7.4 %collective-permute-start.6 = (f32[136,256]{1,0:T(8,128)S(1)}, f32[136,256]{1,0:T(8,128)S(1)}, u32[]{:S(2)}, u32[]{:S(2)}) collective-permute-start(f32[136,256]{1,0:T(8,128)S(1)} %get-tuple-element.67.a), channel_id=1, source_target_pairs={{0,64},{1,65},{2,66},{3,67},{4,68},{5,69},{6,70},{7,71},{8,72},{9,... | collective-permute-start | bytes 417800 | tf_op jit(solution)/shard_map/ppermute | solution.py:326
  90.9 19.2 %collective-permute-start.35 = (f32[4,136,256]{2,1,0:T(8,128)S(1)}, f32[4,136,256]{2,1,0:T(8,128)S(1)}, u32[]{:S(2)}, u32[]{:S(2)}) collective-permute-start(f32[4,136,256]{2,1,0:T(8,128)S(1)} %shard_map.73.p), channel_id=1, source_target_pairs={{0,8},{8,0},{16,24},{24,16},{32,40},{40,32},{48,56},{56,48},{1,9},... | collective-permute-start | bytes 1671176 | tf_op jit(solution)/shard_map/ppermute | solution.py:36
  94.4 7.5 %collective-permute-start.21 = (f32[2,136,256]{2,1,0:T(8,128)S(1)}, f32[2,136,256]{2,1,0:T(8,128)S(1)}, u32[]{:S(2)}, u32[]{:S(2)}) collective-permute-start(f32[2,136,256]{2,1,0:T(8,128)S(1)} %shard_map.59.a), channel_id=1, source_target_pairs={{0,48},{8,24},{16,32},{24,8},{32,16},{40,56},{48,0},{56,40},{1,49}... | collective-permute-start | bytes 835592 | tf_op jit(solution)/shard_map/ppermute | solution.py:32
  94.7 6.8 %collective-permute-start.7 = (f32[136,256]{1,0:T(8,128)S(1)}, f32[136,256]{1,0:T(8,128)S(1)}, u32[]{:S(2)}, u32[]{:S(2)}) collective-permute-start(f32[136,256]{1,0:T(8,128)S(1)} %shard_map.45), channel_id=1, source_target_pairs={{0,16},{8,56},{16,0},{24,40},{32,48},{40,24},{48,32},{56,8},{1,17}... | collective-permute-start | bytes 417800 | tf_op jit(solution)/shard_map/ppermute | solution.py:32
  101.5 5.8 %collective-permute-start.8 = (f32[2,136,256]{2,1,0:T(8,128)S(1)}, f32[2,136,256]{2,1,0:T(8,128)S(1)}, u32[]{:S(2)}, u32[]{:S(2)}) collective-permute-start(f32[2,136,256]{2,1,0:T(8,128)S(1)} %shard_map.46.a), channel_id=1, source_target_pairs={{0,48},{8,24},{16,32},{24,8},{32,16},{40,56},{48,0},{56,40},{1,49}... | collective-permute-start | bytes 835592 | tf_op jit(solution)/shard_map/ppermute | solution.py:32
  101.9 12.7 %collective-permute-start.22 = (f32[4,136,256]{2,1,0:T(8,128)S(1)}, f32[4,136,256]{2,1,0:T(8,128)S(1)}, u32[]{:S(2)}, u32[]{:S(2)}) collective-permute-start(f32[4,136,256]{2,1,0:T(8,128)S(1)} %shard_map.60.p), channel_id=1, source_target_pairs={{0,8},{8,0},{16,24},{24,16},{32,40},{40,32},{48,56},{56,48},{1,9},... | collective-permute-start | bytes 1671176 | tf_op jit(solution)/shard_map/ppermute | solution.py:36
  107.3 13.7 %collective-permute-start.9 = (f32[4,136,256]{2,1,0:T(8,128)S(1)}, f32[4,136,256]{2,1,0:T(8,128)S(1)}, u32[]{:S(2)}, u32[]{:S(2)}) collective-permute-start(f32[4,136,256]{2,1,0:T(8,128)S(1)} %shard_map.47.p), channel_id=1, source_target_pairs={{0,8},{8,0},{16,24},{24,16},{32,40},{40,32},{48,56},{56,48},{1,9},... | collective-permute-start | bytes 1671176 | tf_op jit(solution)/shard_map/ppermute | solution.py:36
  114.1 11.4 %collective-permute-start.36 = (f32[4,136,256]{2,1,0:T(8,128)S(1)}, f32[4,136,256]{2,1,0:T(8,128)S(1)}, u32[]{:S(2)}, u32[]{:S(2)}) collective-permute-start(f32[4,136,256]{2,1,0:T(8,128)S(1)} %get-tuple-element.99), channel_id=1, source_target_pairs={{0,6},{1,7},{2,4},{3,5},{4,2},{5,3},{6,0},{7,1},{8,9},{9,8},{10,11... | collective-permute-start | bytes 1671176 | tf_op jit(solution)/shard_map/ppermute | solution.py:41
  118.7 11.6 %collective-permute-start.23 = (f32[4,136,256]{2,1,0:T(8,128)S(1)}, f32[4,136,256]{2,1,0:T(8,128)S(1)}, u32[]{:S(2)}, u32[]{:S(2)}) collective-permute-start(f32[4,136,256]{2,1,0:T(8,128)S(1)} %get-tuple-element.84), channel_id=1, source_target_pairs={{0,2},{1,3},{2,0},{3,1},{4,6},{5,7},{6,4},{7,5},{8,14},{9,15},{10,... | collective-permute-start | bytes 1671176 | tf_op jit(solution)/shard_map/ppermute | solution.py:41
  125.1 11.3 %collective-permute-start.10 = (f32[4,136,256]{2,1,0:T(8,128)S(1)}, f32[4,136,256]{2,1,0:T(8,128)S(1)}, u32[]{:S(2)}, u32[]{:S(2)}) collective-permute-start(f32[4,136,256]{2,1,0:T(8,128)S(1)} %get-tuple-element.69), channel_id=1, source_target_pairs={{0,1},{1,0},{2,3},{3,2},{4,5},{5,4},{6,7},{7,6},{8,10},{9,11},{10,... | collective-permute-start | bytes 1671176 | tf_op jit(solution)/shard_map/ppermute | solution.py:41
  125.6 13.8 %collective-permute-start.37 = (f32[2,136,256]{2,1,0:T(8,128)S(1)}, f32[2,136,256]{2,1,0:T(8,128)S(1)}, u32[]{:S(2)}, u32[]{:S(2)}) collective-permute-start(f32[2,136,256]{2,1,0:T(8,128)S(1)} %get-tuple-element.101), channel_id=1, source_target_pairs={{0,1},{1,0},{2,3},{3,2},{4,5},{5,4},{6,7},{7,6},{8,10},{9,11},{10,... | collective-permute-start | bytes 835592 | tf_op jit(solution)/shard_map/ppermute | solution.py:41
  130.3 9.2 %collective-permute-start.24 = (f32[2,136,256]{2,1,0:T(8,128)S(1)}, f32[2,136,256]{2,1,0:T(8,128)S(1)}, u32[]{:S(2)}, u32[]{:S(2)}) collective-permute-start(f32[2,136,256]{2,1,0:T(8,128)S(1)} %get-tuple-element.86), channel_id=1, source_target_pairs={{0,6},{1,7},{2,4},{3,5},{4,2},{5,3},{6,0},{7,1},{8,9},{9,8},{10,11... | collective-permute-start | bytes 835592 | tf_op jit(solution)/shard_map/ppermute | solution.py:41
  136.5 7.1 %collective-permute-start.11 = (f32[2,136,256]{2,1,0:T(8,128)S(1)}, f32[2,136,256]{2,1,0:T(8,128)S(1)}, u32[]{:S(2)}, u32[]{:S(2)}) collective-permute-start(f32[2,136,256]{2,1,0:T(8,128)S(1)} %get-tuple-element.71), channel_id=1, source_target_pairs={{0,2},{1,3},{2,0},{3,1},{4,6},{5,7},{6,4},{7,5},{8,14},{9,15},{10,... | collective-permute-start | bytes 835592 | tf_op jit(solution)/shard_map/ppermute | solution.py:41
  139.4 5.7 %collective-permute-start.38 = (f32[1,136,256]{2,1,0:T(8,128)S(1)}, f32[1,136,256]{2,1,0:T(8,128)S(1)}, u32[]{:S(2)}, u32[]{:S(2)}) collective-permute-start(f32[1,136,256]{2,1,0:T(8,128)S(1)} %get-tuple-element.103), channel_id=1, source_target_pairs={{0,2},{1,3},{2,0},{3,1},{4,6},{5,7},{6,4},{7,5},{8,14},{9,15},{10,... | collective-permute-start | bytes 417800 | tf_op jit(solution)/shard_map/ppermute | solution.py:41
  139.6 5.8 %collective-permute-start.25 = (f32[1,136,256]{2,1,0:T(8,128)S(1)}, f32[1,136,256]{2,1,0:T(8,128)S(1)}, u32[]{:S(2)}, u32[]{:S(2)}) collective-permute-start(f32[1,136,256]{2,1,0:T(8,128)S(1)} %get-tuple-element.88), channel_id=1, source_target_pairs={{0,1},{1,0},{2,3},{3,2},{4,5},{5,4},{6,7},{7,6},{8,10},{9,11},{10,... | collective-permute-start | bytes 417800 | tf_op jit(solution)/shard_map/ppermute | solution.py:41
  143.6 5.6 %collective-permute-start.12 = (f32[1,136,256]{2,1,0:T(8,128)S(1)}, f32[1,136,256]{2,1,0:T(8,128)S(1)}, u32[]{:S(2)}, u32[]{:S(2)}) collective-permute-start(f32[1,136,256]{2,1,0:T(8,128)S(1)} %get-tuple-element.73), channel_id=1, source_target_pairs={{0,6},{1,7},{2,4},{3,5},{4,2},{5,3},{6,0},{7,1},{8,9},{9,8},{10,11... | collective-permute-start | bytes 417800 | tf_op jit(solution)/shard_map/ppermute | solution.py:41
where the time goes:
time: 167 us; the launch traced here: 166 us
  starting transfers between devices  58.7 us (35%)
  waiting for transfers between devices  55.9 us (33%)
  Pallas kernels  34 us (20%)
  blocking collectives  15.6 us (9%)
    pallas_call x42, Pallas kernels, call(): pl.pallas_call(body, out_shape=[jax.ShapeDtypeStruct(s, t) for s, t in ou...  34 us
    ppermute x18, waiting for transfers between devices, swap_cols(): return lax.ppermute(value, ('row', 'col'), pairs)  31.5 us
    ppermute x12, waiting for transfers between devices, swap_rows(): return lax.ppermute(value, 'row', pairs)  19.7 us
    ppermute x18, starting transfers between devices, swap_cols(): return lax.ppermute(value, ('row', 'col'), pairs)  17.6 us
    all_to_all x1, blocking collectives, pipeline(): lax.all_to_all(jnp.broadcast_to(lanes[None], (64, *lanes.shape)), ('row',...  15.6 us
    ppermute x3, starting transfers between devices, pipeline(): moved = lax.ppermute(y, 'section', [(0, 1)])  14.3 us
    ppermute x12, starting transfers between devices, swap_rows(): return lax.ppermute(value, 'row', pairs)  13.8 us
    ppermute x6, starting transfers between devices, swap_cores(): return lax.ppermute(value, 'row', [(r, r ^ 1) for r in range(8)])  12.9 us
  transfers between devices with their start and end apart: 39, of which 19 were waited for; matrix products, arithmetic and copies ran while one was open for 0% of the time, Pallas kernels for 20%

commit v1 on v0

--- a/solution.py
+++ b/solution.py
@@ -6,7 +6,7 @@
 from jax.sharding import PartitionSpec as P
 
 
-CHUNKS = (128, 128, 128)
+CHUNKS = (144, 128, 112)
 D = 16384
 F = 256
 f32 = jnp.float32
@@ -62,7 +62,7 @@
 
 
 def split_weights(weights, half):
-    block, slots = 128, 4
+    block, slots = 64, 8
     count = 1024 // block
     per = F // block
 
@@ -167,7 +167,7 @@
             lhs[:rows, m * F : (m + 1) * F] = first
             lhs[rows:, m * F : (m + 1) * F] = (value - first.astype(f32)).astype(bf16)
 
-        def step(k, _):
+        def step(k):
             for target, slot in ((send, k + 4), (keep, k)):
                 spot = pl.ds(pl.multiple_of(place(slot) * F, F), F)
                 both = jnp.dot(lhs[:, :1024], w1[:, spot], preferred_element_type=f32)
@@ -177,7 +177,8 @@
                 target[k, :rows] = both[:rows] + both[rows:] + other
             return 0
 
-        lax.fori_loop(0, 4, step, 0, unroll=2)
+        for k in range(4):
+            step(k)
         if second_layer:
             lanes = rows_to_lanes(total, rows)
             lanes = jnp.concatenate([lanes, jnp.zeros((8, 128), f32)], axis=1)

time: 167 us -> 179 us (1.072)
  starting transfers between devices: 58.7 us -> 79.5 us
  waiting for transfers between devices: 55.9 us -> 47.5 us
  Pallas kernels: 34 us -> 31.2 us
  blocking collectives: 15.6 us -> 17.6 us
    ppermute x6, starting transfers between devices: 12.9 us -> 26.1 us  [swap_cores(): return lax.ppermute(value, 'row', [(r, r ^ 1) for r in range(8)])]
    ppermute x18, waiting for transfers between devices: 31.5 us -> 24.4 us  [swap_cols(): return lax.ppermute(value, ('row', 'col'), pairs)]
    ppermute x18, starting transfers between devices: 17.6 us -> 23.3 us  [swap_cols(): return lax.ppermute(value, ('row', 'col'), pairs)]
    pallas_call x42, Pallas kernels: 34 us -> 31.2 us  [call(): pl.pallas_call(body, out_shape=[jax.ShapeDtypeStruct(s, t) for s, t in ou...]
    all_to_all x1, blocking collectives: 15.6 us -> 17.6 us  [pipeline(): lax.all_to_all(jnp.broadcast_to(lanes[None], (64, *lanes.shape)), ('row',...]
  transfers between devices with their start and end apart: 39 -> 39, of which waited for: 19 -> 15; matrix products, arithmetic and copies ran while one was open for 0% -> 1% of each run, Pallas kernels for 20% -> 17%
where the time goes in v1:
time: 179 us
  starting transfers between devices  79.5 us (44%)
  waiting for transfers between devices  47.5 us (27%)
  Pallas kernels  31.2 us (17%)
  blocking collectives  17.6 us (10%)
  local copies, waits for them, and re-layouts  2.86 us (2%)
    pallas_call x42, Pallas kernels, call(): pl.pallas_call(body, out_shape=[jax.ShapeDtypeStruct(s, t) for s, t in ou...  31.2 us
    ppermute x6, starting transfers between devices, swap_cores(): return lax.ppermute(value, 'row', [(r, r ^ 1) for r in range(8)])  26.1 us
    ppermute x18, waiting for transfers between devices, swap_cols(): return lax.ppermute(value, ('row', 'col'), pairs)  24.4 us
    ppermute x18, starting transfers between devices, swap_cols(): return lax.ppermute(value, ('row', 'col'), pairs)  23.3 us
    ppermute x12, waiting for transfers between devices, swap_rows(): return lax.ppermute(value, 'row', pairs)  19.1 us
    all_to_all x1, blocking collectives, pipeline(): lax.all_to_all(jnp.broadcast_to(lanes[None], (64, *lanes.shape)), ('row',...  17.6 us
    ppermute x12, starting transfers between devices, swap_rows(): return lax.ppermute(value, 'row', pairs)  15.1 us
    ppermute x3, starting transfers between devices, pipeline(): moved = lax.ppermute(y, 'section', [(0, 1)])  15 us
  transfers between devices with their start and end apart: 39, of which 15 were waited for; matrix products, arithmetic and copies ran while one was open for 1% of the time, Pallas kernels for 17%

profile of v1, /device:TPU:1, one launch (start us, length us, event | category | flops | bytes accessed | tf_op | source)
XLA Modules:
  0.0 179.2 jit_solution(8805050317394028903)
XLA Ops:
  0.0 0.9 fusion.2
  0.9 3.4 %collective-permute-start = (f32[144,256]{1,0:T(8,128)S(1)}, f32[144,256]{1,0:T(8,128)S(1)}, u32[]{:S(2)}, u32[]{:S(2)}) collective-permute-start(f32[144,256]{1,0:T(8,128)S(1)} %get-tuple-element.113), channel_id=1, source_target_pairs={{0,16},{8,56},{16,0},{24,40},{32,48},{40,24},{48,32},{56,8},{1,17}... | collective-permute-start | bytes 442376 | tf_op jit(solution)/shard_map/ppermute | solution.py:32
  4.3 2.5 %collective-permute-done = f32[144,256]{1,0:T(8,128)S(1)} collective-permute-done((f32[144,256]{1,0:T(8,128)S(1)}, f32[144,256]{1,0:T(8,128)S(1)}, u32[]{:S(2)}, u32[]{:S(2)}) %collective-permute-start) | collective-permute-done | bytes 147488 | tf_op jit(solution)/shard_map/ppermute | solution.py:32
  7.4 0.9 fusion.1
  8.4 2.3 %collective-permute-start.13 = (f32[128,256]{1,0:T(8,128)S(1)}, f32[128,256]{1,0:T(8,128)S(1)}, u32[]{:S(2)}, u32[]{:S(2)}) collective-permute-start(f32[128,256]{1,0:T(8,128)S(1)} %get-tuple-element.111), channel_id=1, source_target_pairs={{0,16},{8,56},{16,0},{24,40},{32,48},{40,24},{48,32},{56,8},{1,17}... | collective-permute-start | bytes 393224 | tf_op jit(solution)/shard_map/ppermute | solution.py:32
  10.6 4.5 %collective-permute-done.13 = f32[128,256]{1,0:T(8,128)S(1)} collective-permute-done((f32[128,256]{1,0:T(8,128)S(1)}, f32[128,256]{1,0:T(8,128)S(1)}, u32[]{:S(2)}, u32[]{:S(2)}) %collective-permute-start.13) | collective-permute-done | bytes 131104 | tf_op jit(solution)/shard_map/ppermute | solution.py:32
  15.7 2.1 %collective-permute-start.2 = (f32[4,144,256]{2,1,0:T(8,128)S(1)}, f32[4,144,256]{2,1,0:T(8,128)S(1)}, u32[]{:S(2)}, u32[]{:S(2)}) collective-permute-start(f32[4,144,256]{2,1,0:T(8,128)S(1)} %shard_map.38.p), channel_id=1, source_target_pairs={{0,8},{8,0},{16,24},{24,16},{32,40},{40,32},{48,56},{56,48},{1,9},... | collective-permute-start | bytes 1769480 | tf_op jit(solution)/shard_map/ppermute | solution.py:36
  17.8 2.7 %collective-permute-done.14.b = f32[2,128,256]{2,1,0:T(8,128)S(1)} collective-permute-done((f32[2,128,256]{2,1,0:T(8,128)S(1)}, f32[2,128,256]{2,1,0:T(8,128)S(1)}, u32[]{:S(2)}, u32[]{:S(2)}) %collective-permute-start.14) | collective-permute-done | bytes 262176 | tf_op jit(solution)/shard_map/ppermute | solution.py:32
  20.5 3.8 %collective-permute-start.15 = (f32[4,128,256]{2,1,0:T(8,128)S(1)}, f32[4,128,256]{2,1,0:T(8,128)S(1)}, u32[]{:S(2)}, u32[]{:S(2)}) collective-permute-start(f32[4,128,256]{2,1,0:T(8,128)S(1)} %shard_map.53.p), channel_id=1, source_target_pairs={{0,8},{8,0},{16,24},{24,16},{32,40},{40,32},{48,56},{56,48},{1,9},... | collective-permute-start | bytes 1572872 | tf_op jit(solution)/shard_map/ppermute | solution.py:36
  24.3 0.9 fusion
  26.1 3.7 %shard_map.39 = (bf16[1024,2048]{1,0:T(8,128)(2,1)S(1)}, bf16[1024,2048]{1,0:T(8,128)(2,1)S(1)}) custom-call(f32[2048,2048]{1,0:T(8,128)} %bitcast.33), custom_call_target="tpu_custom_call" | custom-call | flops 16777216 | tf_op jit(solution)/shard_map/pallas_call | solution.py:53
  29.8 3.8 %shard_map.40 = (bf16[1024,2048]{1,0:T(8,128)(2,1)S(1)}, bf16[1024,2048]{1,0:T(8,128)(2,1)S(1)}) custom-call(f32[2048,2048]{1,0:T(8,128)} %bitcast.34), custom_call_target="tpu_custom_call" | custom-call | flops 16777216 | tf_op jit(solution)/shard_map/pallas_call | solution.py:53
  33.7 3.9 %shard_map.41 = (f32[4,144,256]{2,1,0:T(8,128)S(1)}, f32[4,144,256]{2,1,0:T(8,128)S(1)}) custom-call(f32[4,144,256]{2,1,0:T(8,128)S(1)} %shard_map.38.p, f32[4,144,256]{2,1,0:T(8,128)S(1)} %collective-permute-done.2.q, bf16[1024,2048]{1,0:T(8,128)(2,1)S(1)} %get-tuple-element.57.w1, bf16[1024,2048]{1,0:T(8,128)(2,1)S(1)} %get-tuple-element.58.w2, ...), custom_call_target="tpu_custom_call" | custom-call | flops 3623878656 | tf_op jit(solution)/shard_map/pallas_call | solution.py:53
  37.7 1.4 collective-permute-start.3
  39.0 3.5 %shard_map.54 = (f32[4,128,256]{2,1,0:T(8,128)S(1)}, f32[4,128,256]{2,1,0:T(8,128)S(1)}) custom-call(f32[4,128,256]{2,1,0:T(8,128)S(1)} %shard_map.53.p, f32[4,128,256]{2,1,0:T(8,128)S(1)} %collective-permute-done.15.q, bf16[1024,2048]{1,0:T(8,128)(2,1)S(1)} %get-tuple-element.57.w1, bf16[1024,2048]{1,0:T(8,128)(2,1)S(1)} %get-tuple-element.58.w2, ...), custom_call_target="tpu_custom_call" | custom-call | flops 3221225472 | tf_op jit(solution)/shard_map/pallas_call | solution.py:53
  42.6 2.0 %collective-permute-start.16 = (f32[4,128,256]{2,1,0:T(8,128)S(1)}, f32[4,128,256]{2,1,0:T(8,128)S(1)}, u32[]{:S(2)}, u32[]{:S(2)}) collective-permute-start(f32[4,128,256]{2,1,0:T(8,128)S(1)} %get-tuple-element.77), channel_id=1, source_target_pairs={{0,2},{1,3},{2,0},{3,1},{4,6},{5,7},{6,4},{7,5},{8,14},{9,15},{10,... | collective-permute-start | bytes 1572872 | tf_op jit(solution)/shard_map/ppermute | solution.py:41
  45.3 6.6 %collective-permute-done.16.got = f32[4,128,256]{2,1,0:T(8,128)S(1)} collective-permute-done((f32[4,128,256]{2,1,0:T(8,128)S(1)}, f32[4,128,256]{2,1,0:T(8,128)S(1)}, u32[]{:S(2)}, u32[]{:S(2)}) %collective-permute-start.16) | collective-permute-done | bytes 524320 | tf_op jit(solution)/shard_map/ppermute | solution.py:41
  51.9 1.7 collective-permute-start.17
  53.7 2.2 %collective-permute-start.4 = (f32[2,144,256]{2,1,0:T(8,128)S(1)}, f32[2,144,256]{2,1,0:T(8,128)S(1)}, u32[]{:S(2)}, u32[]{:S(2)}) collective-permute-start(f32[2,144,256]{2,1,0:T(8,128)S(1)} %get-tuple-element.64), channel_id=1, source_target_pairs={{0,2},{1,3},{2,0},{3,1},{4,6},{5,7},{6,4},{7,5},{8,14},{9,15},{10,... | collective-permute-start | bytes 884744 | tf_op jit(solution)/shard_map/ppermute | solution.py:41
  55.9 3.2 %shard_map.67 = (f32[4,112,256]{2,1,0:T(8,128)S(1)}, f32[4,112,256]{2,1,0:T(8,128)S(1)}) custom-call(f32[4,112,256]{2,1,0:T(8,128)S(1)} %shard_map.66.p, f32[4,112,256]{2,1,0:T(8,128)S(1)} %collective-permute-done.28.q, bf16[1024,2048]{1,0:T(8,128)(2,1)S(1)} %get-tuple-element.57.w1, bf16[1024,2048]{1,0:T(8,128)(2,1)S(1)} %get-tuple-element.58.w2, ...), custom_call_target="tpu_custom_call" | custom-call | flops 2818572288 | tf_op jit(solution)/shard_map/pallas_call | solution.py:53
  59.4 4.3 %collective-permute-done.18.q = f32[1,128,256]{2,1,0:T(8,128)S(1)} collective-permute-done((f32[1,128,256]{2,1,0:T(8,128)S(1)}, f32[1,128,256]{2,1,0:T(8,128)S(1)}, u32[]{:S(2)}, u32[]{:S(2)}) %collective-permute-start.18) | collective-permute-done | bytes 131104 | tf_op jit(solution)/shard_map/ppermute | solution.py:41
  63.8 5.5 %collective-permute-start.19 = (f32[136,256]{1,0:T(8,128)S(1)}, f32[136,256]{1,0:T(8,128)S(1)}, u32[]{:S(2)}, u32[]{:S(2)}) collective-permute-start(f32[136,256]{1,0:T(8,128)S(1)} %get-tuple-element.82.a), channel_id=1, source_target_pairs={{0,64},{1,65},{2,66},{3,67},{4,68},{5,69},{6,70},{7,71},{8,72},{9,... | collective-permute-start | bytes 417800 | tf_op jit(solution)/shard_map/ppermute | solution.py:327
  70.2 1.1 collective-permute-done.19.b
  71.3 2.0 %collective-permute-start.20 = (f32[136,256]{1,0:T(8,128)S(1)}, f32[136,256]{1,0:T(8,128)S(1)}, u32[]{:S(2)}, u32[]{:S(2)}) collective-permute-start(f32[136,256]{1,0:T(8,128)S(1)} %shard_map.58), channel_id=1, source_target_pairs={{0,16},{8,56},{16,0},{24,40},{32,48},{40,24},{48,32},{56,8},{1,17}... | collective-permute-start | bytes 417800 | tf_op jit(solution)/shard_map/ppermute | solution.py:32
  74.1 4.6 %collective-permute-start.6 = (f32[152,256]{1,0:T(8,128)S(1)}, f32[152,256]{1,0:T(8,128)S(1)}, u32[]{:S(2)}, u32[]{:S(2)}) collective-permute-start(f32[152,256]{1,0:T(8,128)S(1)} %get-tuple-element.67.a), channel_id=1, source_target_pairs={{0,64},{1,65},{2,66},{3,67},{4,68},{5,69},{6,70},{7,71},{8,72},{9,... | collective-permute-start | bytes 466952 | tf_op jit(solution)/shard_map/ppermute | solution.py:327
  78.9 0.9 collective-permute-start.21
  79.8 1.0 collective-permute-done.6.b
  81.7 4.5 %collective-permute-done.7 = f32[152,256]{1,0:T(8,128)S(1)} collective-permute-done((f32[152,256]{1,0:T(8,128)S(1)}, f32[152,256]{1,0:T(8,128)S(1)}, u32[]{:S(2)}, u32[]{:S(2)}) %collective-permute-start.7) | collective-permute-done | bytes 155680 | tf_op jit(solution)/shard_map/ppermute | solution.py:32
  86.4 1.1 collective-permute-start.31
  87.5 9.0 %collective-permute-start.22 = (f32[4,136,256]{2,1,0:T(8,128)S(1)}, f32[4,136,256]{2,1,0:T(8,128)S(1)}, u32[]{:S(2)}, u32[]{:S(2)}) collective-permute-start(f32[4,136,256]{2,1,0:T(8,128)S(1)} %shard_map.60.p), channel_id=1, source_target_pairs={{0,8},{8,0},{16,24},{24,16},{32,40},{40,32},{48,56},{56,48},{1,9},... | collective-permute-start | bytes 1671176 | tf_op jit(solution)/shard_map/ppermute | solution.py:36
  96.6 4.9 %collective-permute-start.32 = (f32[120,256]{1,0:T(8,128)S(1)}, f32[120,256]{1,0:T(8,128)S(1)}, u32[]{:S(2)}, u32[]{:S(2)}) collective-permute-start(f32[120,256]{1,0:T(8,128)S(1)} %get-tuple-element.97.a), channel_id=1, source_target_pairs={{0,64},{1,65},{2,66},{3,67},{4,68},{5,69},{6,70},{7,71},{8,72},{9,... | collective-permute-start | bytes 368648 | tf_op jit(solution)/shard_map/ppermute | solution.py:327
  101.5 1.8 %collective-permute-done.32.b = f32[120,256]{1,0:T(8,128)S(1)} collective-permute-done((f32[120,256]{1,0:T(8,128)S(1)}, f32[120,256]{1,0:T(8,128)S(1)}, u32[]{:S(2)}, u32[]{:S(2)}) %collective-permute-start.32) | collective-permute-done | bytes 122912 | tf_op jit(solution)/shard_map/ppermute | solution.py:327
  103.4 1.9 %collective-permute-start.33 = (f32[120,256]{1,0:T(8,128)S(1)}, f32[120,256]{1,0:T(8,128)S(1)}, u32[]{:S(2)}, u32[]{:S(2)}) collective-permute-start(f32[120,256]{1,0:T(8,128)S(1)} %shard_map.71), channel_id=1, source_target_pairs={{0,16},{8,56},{16,0},{24,40},{32,48},{40,24},{48,32},{56,8},{1,17}... | collective-permute-start | bytes 368648 | tf_op jit(solution)/shard_map/ppermute | solution.py:32
  105.3 3.6 %collective-permute-start.9 = (f32[4,152,256]{2,1,0:T(8,128)S(1)}, f32[4,152,256]{2,1,0:T(8,128)S(1)}, u32[]{:S(2)}, u32[]{:S(2)}) collective-permute-start(f32[4,152,256]{2,1,0:T(8,128)S(1)} %shard_map.47.p), channel_id=1, source_target_pairs={{0,8},{8,0},{16,24},{24,16},{32,40},{40,32},{48,56},{56,48},{1,9},... | collective-permute-start | bytes 1867784 | tf_op jit(solution)/shard_map/ppermute | solution.py:36
  108.9 1.8 %collective-permute-start.34 = (f32[2,120,256]{2,1,0:T(8,128)S(1)}, f32[2,120,256]{2,1,0:T(8,128)S(1)}, u32[]{:S(2)}, u32[]{:S(2)}) collective-permute-start(f32[2,120,256]{2,1,0:T(8,128)S(1)} %shard_map.72.a), channel_id=1, source_target_pairs={{0,48},{8,24},{16,32},{24,8},{32,16},{40,56},{48,0},{56,40},{1,49}... | collective-permute-start | bytes 737288 | tf_op jit(solution)/shard_map/ppermute | solution.py:32
  110.7 4.8 %collective-permute-done.34.b = f32[2,120,256]{2,1,0:T(8,128)S(1)} collective-permute-done((f32[2,120,256]{2,1,0:T(8,128)S(1)}, f32[2,120,256]{2,1,0:T(8,128)S(1)}, u32[]{:S(2)}, u32[]{:S(2)}) %collective-permute-start.34) | collective-permute-done | bytes 245792 | tf_op jit(solution)/shard_map/ppermute | solution.py:32
  115.5 6.9 %collective-permute-start.35 = (f32[4,120,256]{2,1,0:T(8,128)S(1)}, f32[4,120,256]{2,1,0:T(8,128)S(1)}, u32[]{:S(2)}, u32[]{:S(2)}) collective-permute-start(f32[4,120,256]{2,1,0:T(8,128)S(1)} %shard_map.73.p), channel_id=1, source_target_pairs={{0,8},{8,0},{16,24},{24,16},{32,40},{40,32},{48,56},{56,48},{1,9},... | collective-permute-start | bytes 1474568 | tf_op jit(solution)/shard_map/ppermute | solution.py:36
  122.5 3.6 %shard_map.61 = (f32[4,136,256]{2,1,0:T(8,128)S(1)}, f32[4,136,256]{2,1,0:T(8,128)S(1)}) custom-call(f32[4,136,256]{2,1,0:T(8,128)S(1)} %shard_map.60.p, f32[4,136,256]{2,1,0:T(8,128)S(1)} %collective-permute-done.22.q, bf16[1024,2048]{1,0:T(8,128)(2,1)S(1)} %get-tuple-element.57.w1, bf16[1024,2048]{1,0:T(8,128)(2,1)S(1)} %get-tuple-element.58.w2, ...), custom_call_target="tpu_custom_call" | custom-call | flops 3221225472 | tf_op jit(solution)/shard_map/pallas_call | solution.py:53
  126.0 4.5 %collective-permute-start.23 = (f32[4,136,256]{2,1,0:T(8,128)S(1)}, f32[4,136,256]{2,1,0:T(8,128)S(1)}, u32[]{:S(2)}, u32[]{:S(2)}) collective-permute-start(f32[4,136,256]{2,1,0:T(8,128)S(1)} %get-tuple-element.84), channel_id=1, source_target_pairs={{0,2},{1,3},{2,0},{3,1},{4,6},{5,7},{6,4},{7,5},{8,14},{9,15},{10,... | collective-permute-start | bytes 1671176 | tf_op jit(solution)/shard_map/ppermute | solution.py:41
  130.5 3.9 %shard_map.48 = (f32[4,152,256]{2,1,0:T(8,128)S(1)}, f32[4,152,256]{2,1,0:T(8,128)S(1)}) custom-call(f32[4,152,256]{2,1,0:T(8,128)S(1)} %shard_map.47.p, f32[4,152,256]{2,1,0:T(8,128)S(1)} %collective-permute-done.9.q, bf16[1024,2048]{1,0:T(8,128)(2,1)S(1)} %get-tuple-element.57.w1, bf16[1024,2048]{1,0:T(8,128)(2,1)S(1)} %get-tuple-element.58.w2, ...), custom_call_target="tpu_custom_call" | custom-call | flops 3623878656 | tf_op jit(solution)/shard_map/pallas_call | solution.py:53
  134.5 3.3 %shard_map.74 = (f32[4,120,256]{2,1,0:T(8,128)S(1)}, f32[4,120,256]{2,1,0:T(8,128)S(1)}) custom-call(f32[4,120,256]{2,1,0:T(8,128)S(1)} %shard_map.73.p, f32[4,120,256]{2,1,0:T(8,128)S(1)} %collective-permute-done.35.q, bf16[1024,2048]{1,0:T(8,128)(2,1)S(1)} %get-tuple-element.57.w1, bf16[1024,2048]{1,0:T(8,128)(2,1)S(1)} %get-tuple-element.58.w2, ...), custom_call_target="tpu_custom_call" | custom-call | flops 2818572288 | tf_op jit(solution)/shard_map/pallas_call | solution.py:53
  137.9 6.0 %collective-permute-done.10.got = f32[4,152,256]{2,1,0:T(8,128)S(1)} collective-permute-done((f32[4,152,256]{2,1,0:T(8,128)S(1)}, f32[4,152,256]{2,1,0:T(8,128)S(1)}, u32[]{:S(2)}, u32[]{:S(2)}) %collective-permute-start.10) | collective-permute-done | bytes 622624 | tf_op jit(solution)/shard_map/ppermute | solution.py:41
  144.0 2.5 %collective-permute-start.11 = (f32[2,152,256]{2,1,0:T(8,128)S(1)}, f32[2,152,256]{2,1,0:T(8,128)S(1)}, u32[]{:S(2)}, u32[]{:S(2)}) collective-permute-start(f32[2,152,256]{2,1,0:T(8,128)S(1)} %get-tuple-element.71), channel_id=1, source_target_pairs={{0,2},{1,3},{2,0},{3,1},{4,6},{5,7},{6,4},{7,5},{8,14},{9,15},{10,... | collective-permute-start | bytes 933896 | tf_op jit(solution)/shard_map/ppermute | solution.py:41
  147.5 3.5 %collective-permute-done.11.got = f32[2,152,256]{2,1,0:T(8,128)S(1)} collective-permute-done((f32[2,152,256]{2,1,0:T(8,128)S(1)}, f32[2,152,256]{2,1,0:T(8,128)S(1)}, u32[]{:S(2)}, u32[]{:S(2)}) %collective-permute-start.11) | collective-permute-done | bytes 311328 | tf_op jit(solution)/shard_map/ppermute | solution.py:41
  151.1 0.9 collective-permute-done.24.got
  152.2 5.7 %collective-permute-start.38 = (f32[1,120,256]{2,1,0:T(8,128)S(1)}, f32[1,120,256]{2,1,0:T(8,128)S(1)}, u32[]{:S(2)}, u32[]{:S(2)}) collective-permute-start(f32[1,120,256]{2,1,0:T(8,128)S(1)} %get-tuple-element.103), channel_id=1, source_target_pairs={{0,2},{1,3},{2,0},{3,1},{4,6},{5,7},{6,4},{7,5},{8,14},{9,15},{10,... | collective-permute-start | bytes 368648 | tf_op jit(solution)/shard_map/ppermute | solution.py:41
  157.9 2.3 %collective-permute-done.38.q = f32[1,120,256]{2,1,0:T(8,128)S(1)} collective-permute-done((f32[1,120,256]{2,1,0:T(8,128)S(1)}, f32[1,120,256]{2,1,0:T(8,128)S(1)}, u32[]{:S(2)}, u32[]{:S(2)}) %collective-permute-start.38) | collective-permute-done | bytes 122912 | tf_op jit(solution)/shard_map/ppermute | solution.py:41
  160.8 17.6 %all_to_all.5 = f32[64,1,512]{2,1,0:T(1,128)S(1)} all-to-all(f32[64,1,512]{2,1,0:T(1,128)S(1)} %broadcast_in_dim.9), channel_id=1, replica_groups=mesh['section'=2,'row'=8,'col'=8] {'row','col'}, dimensions={0} | all-to-all | bytes 262144 | tf_op jit(solution)/shard_map/all_to_all | solution.py:338
  (84 shorter events, 9.2 us)
Async XLA Ops:
  0.9 5.9 %collective-permute-start = (f32[144,256]{1,0:T(8,128)S(1)}, f32[144,256]{1,0:T(8,128)S(1)}, u32[]{:S(2)}, u32[]{:S(2)}) collective-permute-start(f32[144,256]{1,0:T(8,128)S(1)} %get-tuple-element.113), channel_id=1, source_target_pairs={{0,16},{8,56},{16,0},{24,40},{32,48},{40,24},{48,32},{56,8},{1,17}... | collective-permute-start | bytes 442376 | tf_op jit(solution)/shard_map/ppermute | solution.py:32
  6.9 8.8 %collective-permute-start.1 = (f32[2,144,256]{2,1,0:T(8,128)S(1)}, f32[2,144,256]{2,1,0:T(8,128)S(1)}, u32[]{:S(2)}, u32[]{:S(2)}) collective-permute-start(f32[2,144,256]{2,1,0:T(8,128)S(1)} %shard_map.37.a), channel_id=1, source_target_pairs={{0,48},{8,24},{16,32},{24,8},{32,16},{40,56},{48,0},{56,40},{1,49}... | collective-permute-start | bytes 884744 | tf_op jit(solution)/shard_map/ppermute | solution.py:32
  8.4 6.8 %collective-permute-start.13 = (f32[128,256]{1,0:T(8,128)S(1)}, f32[128,256]{1,0:T(8,128)S(1)}, u32[]{:S(2)}, u32[]{:S(2)}) collective-permute-start(f32[128,256]{1,0:T(8,128)S(1)} %get-tuple-element.111), channel_id=1, source_target_pairs={{0,16},{8,56},{16,0},{24,40},{32,48},{40,24},{48,32},{56,8},{1,17}... | collective-permute-start | bytes 393224 | tf_op jit(solution)/shard_map/ppermute | solution.py:32
  15.2 5.3 %collective-permute-start.14 = (f32[2,128,256]{2,1,0:T(8,128)S(1)}, f32[2,128,256]{2,1,0:T(8,128)S(1)}, u32[]{:S(2)}, u32[]{:S(2)}) collective-permute-start(f32[2,128,256]{2,1,0:T(8,128)S(1)} %shard_map.52.a), channel_id=1, source_target_pairs={{0,48},{8,24},{16,32},{24,8},{32,16},{40,56},{48,0},{56,40},{1,49}... | collective-permute-start | bytes 786440 | tf_op jit(solution)/shard_map/ppermute | solution.py:32
  15.7 18.1 %collective-permute-start.2 = (f32[4,144,256]{2,1,0:T(8,128)S(1)}, f32[4,144,256]{2,1,0:T(8,128)S(1)}, u32[]{:S(2)}, u32[]{:S(2)}) collective-permute-start(f32[4,144,256]{2,1,0:T(8,128)S(1)} %shard_map.38.p), channel_id=1, source_target_pairs={{0,8},{8,0},{16,24},{24,16},{32,40},{40,32},{48,56},{56,48},{1,9},... | collective-permute-start | bytes 1769480 | tf_op jit(solution)/shard_map/ppermute | solution.py:36
  20.5 18.5 %collective-permute-start.15 = (f32[4,128,256]{2,1,0:T(8,128)S(1)}, f32[4,128,256]{2,1,0:T(8,128)S(1)}, u32[]{:S(2)}, u32[]{:S(2)}) collective-permute-start(f32[4,128,256]{2,1,0:T(8,128)S(1)} %shard_map.53.p), channel_id=1, source_target_pairs={{0,8},{8,0},{16,24},{24,16},{32,40},{40,32},{48,56},{56,48},{1,9},... | collective-permute-start | bytes 1572872 | tf_op jit(solution)/shard_map/ppermute | solution.py:36
  25.2 8.4 %collective-permute-start.26 = (f32[112,256]{1,0:T(8,128)S(1)}, f32[112,256]{1,0:T(8,128)S(1)}, u32[]{:S(2)}, u32[]{:S(2)}) collective-permute-start(f32[112,256]{1,0:T(8,128)S(1)} %get-tuple-element.109), channel_id=1, source_target_pairs={{0,16},{8,56},{16,0},{24,40},{32,48},{40,24},{48,32},{56,8},{1,17}... | collective-permute-start | bytes 344072 | tf_op jit(solution)/shard_map/ppermute | solution.py:32
  33.6 10.9 %collective-permute-start.27 = (f32[2,112,256]{2,1,0:T(8,128)S(1)}, f32[2,112,256]{2,1,0:T(8,128)S(1)}, u32[]{:S(2)}, u32[]{:S(2)}) collective-permute-start(f32[2,112,256]{2,1,0:T(8,128)S(1)} %shard_map.65.a), channel_id=1, source_target_pairs={{0,48},{8,24},{16,32},{24,8},{32,16},{40,56},{48,0},{56,40},{1,49}... | collective-permute-start | bytes 688136 | tf_op jit(solution)/shard_map/ppermute | solution.py:32
  37.7 16.0 %collective-permute-start.3 = (f32[4,144,256]{2,1,0:T(8,128)S(1)}, f32[4,144,256]{2,1,0:T(8,128)S(1)}, u32[]{:S(2)}, u32[]{:S(2)}) collective-permute-start(f32[4,144,256]{2,1,0:T(8,128)S(1)} %get-tuple-element.62), channel_id=1, source_target_pairs={{0,1},{1,0},{2,3},{3,2},{4,5},{5,4},{6,7},{7,6},{8,10},{9,11},{10,... | collective-permute-start | bytes 1769480 | tf_op jit(solution)/shard_map/ppermute | solution.py:41
  42.6 9.3 %collective-permute-start.16 = (f32[4,128,256]{2,1,0:T(8,128)S(1)}, f32[4,128,256]{2,1,0:T(8,128)S(1)}, u32[]{:S(2)}, u32[]{:S(2)}) collective-permute-start(f32[4,128,256]{2,1,0:T(8,128)S(1)} %get-tuple-element.77), channel_id=1, source_target_pairs={{0,2},{1,3},{2,0},{3,1},{4,6},{5,7},{6,4},{7,5},{8,14},{9,15},{10,... | collective-permute-start | bytes 1572872 | tf_op jit(solution)/shard_map/ppermute | solution.py:41
  44.6 11.3 %collective-permute-start.28 = (f32[4,112,256]{2,1,0:T(8,128)S(1)}, f32[4,112,256]{2,1,0:T(8,128)S(1)}, u32[]{:S(2)}, u32[]{:S(2)}) collective-permute-start(f32[4,112,256]{2,1,0:T(8,128)S(1)} %shard_map.66.p), channel_id=1, source_target_pairs={{0,8},{8,0},{16,24},{24,16},{32,40},{40,32},{48,56},{56,48},{1,9},... | collective-permute-start | bytes 1376264 | tf_op jit(solution)/shard_map/ppermute | solution.py:36
  51.9 7.3 %collective-permute-start.17 = (f32[2,128,256]{2,1,0:T(8,128)S(1)}, f32[2,128,256]{2,1,0:T(8,128)S(1)}, u32[]{:S(2)}, u32[]{:S(2)}) collective-permute-start(f32[2,128,256]{2,1,0:T(8,128)S(1)} %get-tuple-element.79), channel_id=1, source_target_pairs={{0,6},{1,7},{2,4},{3,5},{4,2},{5,3},{6,0},{7,1},{8,9},{9,8},{10,11... | collective-permute-start | bytes 786440 | tf_op jit(solution)/shard_map/ppermute | solution.py:41
  53.7 10.0 %copy-start = (f32[1,256]{1,0:T(1,128)S(1)}, f32[1,256]{1,0:T(1,128)}, u32[]{:S(2)}) copy-start(f32[1,256]{1,0:T(1,128)} %g.11) | copy-start | bytes 3076
  53.7 15.6 %collective-permute-start.4 = (f32[2,144,256]{2,1,0:T(8,128)S(1)}, f32[2,144,256]{2,1,0:T(8,128)S(1)}, u32[]{:S(2)}, u32[]{:S(2)}) collective-permute-start(f32[2,144,256]{2,1,0:T(8,128)S(1)} %get-tuple-element.64), channel_id=1, source_target_pairs={{0,2},{1,3},{2,0},{3,1},{4,6},{5,7},{6,4},{7,5},{8,14},{9,15},{10,... | collective-permute-start | bytes 884744 | tf_op jit(solution)/shard_map/ppermute | solution.py:41
  59.1 19.5 %collective-permute-start.29 = (f32[4,112,256]{2,1,0:T(8,128)S(1)}, f32[4,112,256]{2,1,0:T(8,128)S(1)}, u32[]{:S(2)}, u32[]{:S(2)}) collective-permute-start(f32[4,112,256]{2,1,0:T(8,128)S(1)} %get-tuple-element.92), channel_id=1, source_target_pairs={{0,6},{1,7},{2,4},{3,5},{4,2},{5,3},{6,0},{7,1},{8,9},{9,8},{10,11... | collective-permute-start | bytes 1376264 | tf_op jit(solution)/shard_map/ppermute | solution.py:41
  59.3 4.4 %collective-permute-start.18 = (f32[1,128,256]{2,1,0:T(8,128)S(1)}, f32[1,128,256]{2,1,0:T(8,128)S(1)}, u32[]{:S(2)}, u32[]{:S(2)}) collective-permute-start(f32[1,128,256]{2,1,0:T(8,128)S(1)} %get-tuple-element.81), channel_id=1, source_target_pairs={{0,1},{1,0},{2,3},{3,2},{4,5},{5,4},{6,7},{7,6},{8,10},{9,11},{10,... | collective-permute-start | bytes 393224 | tf_op jit(solution)/shard_map/ppermute | solution.py:41
  63.8 7.5 %collective-permute-start.19 = (f32[136,256]{1,0:T(8,128)S(1)}, f32[136,256]{1,0:T(8,128)S(1)}, u32[]{:S(2)}, u32[]{:S(2)}) collective-permute-start(f32[136,256]{1,0:T(8,128)S(1)} %get-tuple-element.82.a), channel_id=1, source_target_pairs={{0,64},{1,65},{2,66},{3,67},{4,68},{5,69},{6,70},{7,71},{8,72},{9,... | collective-permute-start | bytes 417800 | tf_op jit(solution)/shard_map/ppermute | solution.py:327
  69.4 4.7 %collective-permute-start.5 = (f32[1,144,256]{2,1,0:T(8,128)S(1)}, f32[1,144,256]{2,1,0:T(8,128)S(1)}, u32[]{:S(2)}, u32[]{:S(2)}) collective-permute-start(f32[1,144,256]{2,1,0:T(8,128)S(1)} %get-tuple-element.66), channel_id=1, source_target_pairs={{0,6},{1,7},{2,4},{3,5},{4,2},{5,3},{6,0},{7,1},{8,9},{9,8},{10,11... | collective-permute-start | bytes 442376 | tf_op jit(solution)/shard_map/ppermute | solution.py:41
  71.3 7.5 %collective-permute-start.20 = (f32[136,256]{1,0:T(8,128)S(1)}, f32[136,256]{1,0:T(8,128)S(1)}, u32[]{:S(2)}, u32[]{:S(2)}) collective-permute-start(f32[136,256]{1,0:T(8,128)S(1)} %shard_map.58), channel_id=1, source_target_pairs={{0,16},{8,56},{16,0},{24,40},{32,48},{40,24},{48,32},{56,8},{1,17}... | collective-permute-start | bytes 417800 | tf_op jit(solution)/shard_map/ppermute | solution.py:32
  74.1 6.7 %collective-permute-start.6 = (f32[152,256]{1,0:T(8,128)S(1)}, f32[152,256]{1,0:T(8,128)S(1)}, u32[]{:S(2)}, u32[]{:S(2)}) collective-permute-start(f32[152,256]{1,0:T(8,128)S(1)} %get-tuple-element.67.a), channel_id=1, source_target_pairs={{0,64},{1,65},{2,66},{3,67},{4,68},{5,69},{6,70},{7,71},{8,72},{9,... | collective-permute-start | bytes 466952 | tf_op jit(solution)/shard_map/ppermute | solution.py:327
  78.7 7.6 %collective-permute-start.30 = (f32[2,112,256]{2,1,0:T(8,128)S(1)}, f32[2,112,256]{2,1,0:T(8,128)S(1)}, u32[]{:S(2)}, u32[]{:S(2)}) collective-permute-start(f32[2,112,256]{2,1,0:T(8,128)S(1)} %get-tuple-element.94), channel_id=1, source_target_pairs={{0,1},{1,0},{2,3},{3,2},{4,5},{5,4},{6,7},{7,6},{8,10},{9,11},{10,... | collective-permute-start | bytes 688136 | tf_op jit(solution)/shard_map/ppermute | solution.py:41
  78.9 8.6 %collective-permute-start.21 = (f32[2,136,256]{2,1,0:T(8,128)S(1)}, f32[2,136,256]{2,1,0:T(8,128)S(1)}, u32[]{:S(2)}, u32[]{:S(2)}) collective-permute-start(f32[2,136,256]{2,1,0:T(8,128)S(1)} %shard_map.59.a), channel_id=1, source_target_pairs={{0,48},{8,24},{16,32},{24,8},{32,16},{40,56},{48,0},{56,40},{1,49}... | collective-permute-start | bytes 835592 | tf_op jit(solution)/shard_map/ppermute | solution.py:32
  80.8 5.4 %collective-permute-start.7 = (f32[152,256]{1,0:T(8,128)S(1)}, f32[152,256]{1,0:T(8,128)S(1)}, u32[]{:S(2)}, u32[]{:S(2)}) collective-permute-start(f32[152,256]{1,0:T(8,128)S(1)} %shard_map.45), channel_id=1, source_target_pairs={{0,16},{8,56},{16,0},{24,40},{32,48},{40,24},{48,32},{56,8},{1,17}... | collective-permute-start | bytes 466952 | tf_op jit(solution)/shard_map/ppermute | solution.py:32
  86.2 19.0 %collective-permute-start.8 = (f32[2,152,256]{2,1,0:T(8,128)S(1)}, f32[2,152,256]{2,1,0:T(8,128)S(1)}, u32[]{:S(2)}, u32[]{:S(2)}) collective-permute-start(f32[2,152,256]{2,1,0:T(8,128)S(1)} %shard_map.46.a), channel_id=1, source_target_pairs={{0,48},{8,24},{16,32},{24,8},{32,16},{40,56},{48,0},{56,40},{1,49}... | collective-permute-start | bytes 933896 | tf_op jit(solution)/shard_map/ppermute | solution.py:32
  86.4 10.2 %collective-permute-start.31 = (f32[1,112,256]{2,1,0:T(8,128)S(1)}, f32[1,112,256]{2,1,0:T(8,128)S(1)}, u32[]{:S(2)}, u32[]{:S(2)}) collective-permute-start(f32[1,112,256]{2,1,0:T(8,128)S(1)} %get-tuple-element.96), channel_id=1, source_target_pairs={{0,2},{1,3},{2,0},{3,1},{4,6},{5,7},{6,4},{7,5},{8,14},{9,15},{10,... | collective-permute-start | bytes 344072 | tf_op jit(solution)/shard_map/ppermute | solution.py:41
  87.5 35.0 %collective-permute-start.22 = (f32[4,136,256]{2,1,0:T(8,128)S(1)}, f32[4,136,256]{2,1,0:T(8,128)S(1)}, u32[]{:S(2)}, u32[]{:S(2)}) collective-permute-start(f32[4,136,256]{2,1,0:T(8,128)S(1)} %shard_map.60.p), channel_id=1, source_target_pairs={{0,8},{8,0},{16,24},{24,16},{32,40},{40,32},{48,56},{56,48},{1,9},... | collective-permute-start | bytes 1671176 | tf_op jit(solution)/shard_map/ppermute | solution.py:36
  96.6 6.8 %collective-permute-start.32 = (f32[120,256]{1,0:T(8,128)S(1)}, f32[120,256]{1,0:T(8,128)S(1)}, u32[]{:S(2)}, u32[]{:S(2)}) collective-permute-start(f32[120,256]{1,0:T(8,128)S(1)} %get-tuple-element.97.a), channel_id=1, source_target_pairs={{0,64},{1,65},{2,66},{3,67},{4,68},{5,69},{6,70},{7,71},{8,72},{9,... | collective-permute-start | bytes 368648 | tf_op jit(solution)/shard_map/ppermute | solution.py:327
  103.4 5.5 %collective-permute-start.33 = (f32[120,256]{1,0:T(8,128)S(1)}, f32[120,256]{1,0:T(8,128)S(1)}, u32[]{:S(2)}, u32[]{:S(2)}) collective-permute-start(f32[120,256]{1,0:T(8,128)S(1)} %shard_map.71), channel_id=1, source_target_pairs={{0,16},{8,56},{16,0},{24,40},{32,48},{40,24},{48,32},{56,8},{1,17}... | collective-permute-start | bytes 368648 | tf_op jit(solution)/shard_map/ppermute | solution.py:32
  105.3 25.2 %collective-permute-start.9 = (f32[4,152,256]{2,1,0:T(8,128)S(1)}, f32[4,152,256]{2,1,0:T(8,128)S(1)}, u32[]{:S(2)}, u32[]{:S(2)}) collective-permute-start(f32[4,152,256]{2,1,0:T(8,128)S(1)} %shard_map.47.p), channel_id=1, source_target_pairs={{0,8},{8,0},{16,24},{24,16},{32,40},{40,32},{48,56},{56,48},{1,9},... | collective-permute-start | bytes 1867784 | tf_op jit(solution)/shard_map/ppermute | solution.py:36
  108.9 6.6 %collective-permute-start.34 = (f32[2,120,256]{2,1,0:T(8,128)S(1)}, f32[2,120,256]{2,1,0:T(8,128)S(1)}, u32[]{:S(2)}, u32[]{:S(2)}) collective-permute-start(f32[2,120,256]{2,1,0:T(8,128)S(1)} %shard_map.72.a), channel_id=1, source_target_pairs={{0,48},{8,24},{16,32},{24,8},{32,16},{40,56},{48,0},{56,40},{1,49}... | collective-permute-start | bytes 737288 | tf_op jit(solution)/shard_map/ppermute | solution.py:32
  115.5 19.0 %collective-permute-start.35 = (f32[4,120,256]{2,1,0:T(8,128)S(1)}, f32[4,120,256]{2,1,0:T(8,128)S(1)}, u32[]{:S(2)}, u32[]{:S(2)}) collective-permute-start(f32[4,120,256]{2,1,0:T(8,128)S(1)} %shard_map.73.p), channel_id=1, source_target_pairs={{0,8},{8,0},{16,24},{24,16},{32,40},{40,32},{48,56},{56,48},{1,9},... | collective-permute-start | bytes 1474568 | tf_op jit(solution)/shard_map/ppermute | solution.py:36
  126.0 20.4 %collective-permute-start.23 = (f32[4,136,256]{2,1,0:T(8,128)S(1)}, f32[4,136,256]{2,1,0:T(8,128)S(1)}, u32[]{:S(2)}, u32[]{:S(2)}) collective-permute-start(f32[4,136,256]{2,1,0:T(8,128)S(1)} %get-tuple-element.84), channel_id=1, source_target_pairs={{0,2},{1,3},{2,0},{3,1},{4,6},{5,7},{6,4},{7,5},{8,14},{9,15},{10,... | collective-permute-start | bytes 1671176 | tf_op jit(solution)/shard_map/ppermute | solution.py:41
  134.4 9.5 %collective-permute-start.10 = (f32[4,152,256]{2,1,0:T(8,128)S(1)}, f32[4,152,256]{2,1,0:T(8,128)S(1)}, u32[]{:S(2)}, u32[]{:S(2)}) collective-permute-start(f32[4,152,256]{2,1,0:T(8,128)S(1)} %get-tuple-element.69), channel_id=1, source_target_pairs={{0,1},{1,0},{2,3},{3,2},{4,5},{5,4},{6,7},{7,6},{8,10},{9,11},{10,... | collective-permute-start | bytes 1867784 | tf_op jit(solution)/shard_map/ppermute | solution.py:41
  137.8 8.8 %collective-permute-start.36 = (f32[4,120,256]{2,1,0:T(8,128)S(1)}, f32[4,120,256]{2,1,0:T(8,128)S(1)}, u32[]{:S(2)}, u32[]{:S(2)}) collective-permute-start(f32[4,120,256]{2,1,0:T(8,128)S(1)} %get-tuple-element.99), channel_id=1, source_target_pairs={{0,6},{1,7},{2,4},{3,5},{4,2},{5,3},{6,0},{7,1},{8,9},{9,8},{10,11... | collective-permute-start | bytes 1474568 | tf_op jit(solution)/shard_map/ppermute | solution.py:41
  144.0 7.0 %collective-permute-start.11 = (f32[2,152,256]{2,1,0:T(8,128)S(1)}, f32[2,152,256]{2,1,0:T(8,128)S(1)}, u32[]{:S(2)}, u32[]{:S(2)}) collective-permute-start(f32[2,152,256]{2,1,0:T(8,128)S(1)} %get-tuple-element.71), channel_id=1, source_target_pairs={{0,2},{1,3},{2,0},{3,1},{4,6},{5,7},{6,4},{7,5},{8,14},{9,15},{10,... | collective-permute-start | bytes 933896 | tf_op jit(solution)/shard_map/ppermute | solution.py:41
  146.5 5.5 %collective-permute-start.24 = (f32[2,136,256]{2,1,0:T(8,128)S(1)}, f32[2,136,256]{2,1,0:T(8,128)S(1)}, u32[]{:S(2)}, u32[]{:S(2)}) collective-permute-start(f32[2,136,256]{2,1,0:T(8,128)S(1)} %get-tuple-element.86), channel_id=1, source_target_pairs={{0,6},{1,7},{2,4},{3,5},{4,2},{5,3},{6,0},{7,1},{8,9},{9,8},{10,11... | collective-permute-start | bytes 835592 | tf_op jit(solution)/shard_map/ppermute | solution.py:41
  146.7 5.4 %collective-permute-start.37 = (f32[2,120,256]{2,1,0:T(8,128)S(1)}, f32[2,120,256]{2,1,0:T(8,128)S(1)}, u32[]{:S(2)}, u32[]{:S(2)}) collective-permute-start(f32[2,120,256]{2,1,0:T(8,128)S(1)} %get-tuple-element.101), channel_id=1, source_target_pairs={{0,1},{1,0},{2,3},{3,2},{4,5},{5,4},{6,7},{7,6},{8,10},{9,11},{10,... | collective-permute-start | bytes 737288 | tf_op jit(solution)/shard_map/ppermute | solution.py:41
  151.0 9.5 %collective-permute-start.12 = (f32[1,152,256]{2,1,0:T(8,128)S(1)}, f32[1,152,256]{2,1,0:T(8,128)S(1)}, u32[]{:S(2)}, u32[]{:S(2)}) collective-permute-start(f32[1,152,256]{2,1,0:T(8,128)S(1)} %get-tuple-element.73), channel_id=1, source_target_pairs={{0,6},{1,7},{2,4},{3,5},{4,2},{5,3},{6,0},{7,1},{8,9},{9,8},{10,11... | collective-permute-start | bytes 466952 | tf_op jit(solution)/shard_map/ppermute | solution.py:41
  152.0 8.3 %collective-permute-start.25 = (f32[1,136,256]{2,1,0:T(8,128)S(1)}, f32[1,136,256]{2,1,0:T(8,128)S(1)}, u32[]{:S(2)}, u32[]{:S(2)}) collective-permute-start(f32[1,136,256]{2,1,0:T(8,128)S(1)} %get-tuple-element.88), channel_id=1, source_target_pairs={{0,1},{1,0},{2,3},{3,2},{4,5},{5,4},{6,7},{7,6},{8,10},{9,11},{10,... | collective-permute-start | bytes 417800 | tf_op jit(solution)/shard_map/ppermute | solution.py:41
  152.2 7.9 %collective-permute-start.38 = (f32[1,120,256]{2,1,0:T(8,128)S(1)}, f32[1,120,256]{2,1,0:T(8,128)S(1)}, u32[]{:S(2)}, u32[]{:S(2)}) collective-permute-start(f32[1,120,256]{2,1,0:T(8,128)S(1)} %get-tuple-element.103), channel_id=1, source_target_pairs={{0,2},{1,3},{2,0},{3,1},{4,6},{5,7},{6,4},{7,5},{8,14},{9,15},{10,... | collective-permute-start | bytes 368648 | tf_op jit(solution)/shard_map/ppermute | solution.py:41
